TPU v7x, 32 devices: a whole 2x2x4 slice. The times are simulated.
32 devices in a mesh: dp: 4 (over y, x), key: 4 (over z), tensor: 2 (over core).
Axes of the slice: x: 2, y: 2, z: 4, core: 2. Of those that a mesh axis runs over, the one named last changes fastest.
Arguments:
- queries: bfloat16 [4096, 8, 2, 256], P(('dp', 'key'), 'tensor'), may hold values from -6 to 6
- sub_keys: bfloat16 [1024, 8, 2, 256], P('key', 'tensor'), may hold values from -6 to 6
- query_weight: bfloat16 [4096, 4096], P(None, 'tensor'), may hold values from -0.09375 to 0.09375
- sub_choice: int32 [4096, 8, 2, 32], P(('dp', 'key'), 'tensor'), may hold values from 0 to 1023, all different within a row
- pair_choice: int32 [4096, 8, 32], P(('dp', 'key'), 'tensor'), may hold values from 0 to 1023, all different within a row
- weights: float32 [4096, 8, 32], P(('dp', 'key'), 'tensor'), may hold values from 0 to 1, as said below
- weight_grad: float32 [4096, 8, 32], P(('dp', 'key'), 'tensor'), may hold values from -6 to 6
Outputs:
- sub_key_grad: float32 [1024, 8, 2, 256], P(('dp', 'key'), 'tensor')
- input_grad: bfloat16 [4096, 4096], P(('dp', 'key', 'tensor'))
Inputs may be any that keep to these rules, and one draw needn't show every extreme that they name: Each row of weights is positive and sums to one.
All inputs are finite; a program needn't handle non-finite values.
Results may differ from a plain program's by a relative error of at most 0.0058.
Values may be sent and summed in bfloat16 or wider, within the bound.
No kernel may reach another device: no remote copies, remote signals or barrier semaphores. Data moves between devices by JAX's collectives and lax.ppermute only.
A program may use at most 128 MiB of HBM per device.

v0:
```python
import math

import jax
import jax.numpy as jnp
from jax import lax
from jax.sharding import PartitionSpec as P


def on_device(queries, sub_keys, query_weight, sub_choice, pair_choice, weights, weight_grad):
    tok, heads_here, halves, width = queries.shape
    topk = pair_choice.shape[2]
    nsub = sub_keys.shape[0] * lax.axis_size("key")
    score_grad = weights * (weight_grad - jnp.sum(weights * weight_grad, axis=-1, keepdims=True))
    slots = jnp.arange(topk, dtype=jnp.int32)
    first = pair_choice // topk
    second = pair_choice % topk
    grad_one = jnp.sum(
        score_grad[..., None] * (first[..., None] == slots).astype(jnp.float32), axis=2
    )
    grad_two = jnp.sum(
        score_grad[..., None] * (second[..., None] == slots).astype(jnp.float32), axis=2
    )
    slot_grad = jnp.stack([grad_one, grad_two], axis=2)
    count = tok * heads_here * halves
    lines_blk = math.gcd(count, 128)
    line_blocks = count // lines_blk
    row_ids = jnp.arange(nsub, dtype=jnp.int32)
    idx_blocks = sub_choice.reshape(line_blocks, lines_blk, topk)
    val_blocks = slot_grad.reshape(line_blocks, lines_blk, topk)

    def build_rows(pieces):
        idx_here, val_here = pieces
        match = idx_here[:, :, None] == row_ids[None, None, :]
        return jnp.sum(jnp.where(match, val_here[:, :, None], 0.0), axis=1).astype(jnp.bfloat16)

    table = lax.map(build_rows, (idx_blocks, val_blocks)).reshape(tok, heads_here, halves, nsub)
    part_rows = table
    query_grad = jnp.einsum(
        "thxr,rhxf->thxf",
        part_rows,
        lax.all_gather(sub_keys, "key", axis=0, tiled=True),
        preferred_element_type=jnp.float32,
    ).astype(jnp.bfloat16)
    part_rows = table
    partial_value = lax.psum_scatter(
        jnp.einsum("thxr,thxf->rhxf", part_rows, queries, preferred_element_type=jnp.float32),
        "dp",
        scatter_dimension=0,
        tiled=True,
    )
    sub_key_grad = lax.psum_scatter(partial_value, "key", scatter_dimension=0, tiled=True)
    flat = query_grad.reshape(tok, heads_here * halves * width)
    part_rows = flat
    input_grad = lax.psum_scatter(
        lax.dot_general(
            part_rows, query_weight, (((1,), (1,)), ((), ())), preferred_element_type=jnp.float32
        ),
        "tensor",
        scatter_dimension=0,
        tiled=True,
    )
    return (sub_key_grad, input_grad.astype(jnp.bfloat16))


def solution(mesh):
    in_specs = (
        P(("dp", "key"), "tensor", None, None),
        P("key", "tensor", None, None),
        P(None, "tensor"),
        P(("dp", "key"), "tensor", None, None),
        P(("dp", "key"), "tensor", None),
        P(("dp", "key"), "tensor", None),
        P(("dp", "key"), "tensor", None),
    )
    out_specs = (P(("dp", "key"), "tensor", None, None), P(("dp", "key", "tensor"), None))
    return jax.shard_map(
        on_device, mesh=mesh, in_specs=in_specs, out_specs=out_specs, check_vma=False
    )
```

profile of v0, /device:TPU:0, one launch (start us, length us, event | category | flops | bytes accessed | tf_op | source)
XLA Modules:
  0.0 266.0 jit_solution(6091022026719151953)
XLA Ops:
  8.1 3.7 %copy.50 = bf16[256,4,2,256]{0,3,2,1:T(8,128)(2,1)} copy(bf16[256,4,2,256]{3,2,1,0:T(2,128)(2,1)} %param.10) | data formatting | bytes 2097152 | tf_op args[1]
  16.6 71.4 %while.11 = (s32[]{:T(128)}, bf16[16,128,1024]{2,1,0:T(8,128)(2,1)}, s32[16,128,32]{2,1,0:T(8,128)S(1)}, f32[16,128,32]{2,1,0:T(8,128)S(1)}, s32[]{:T(128)}) while((s32[]{:T(128)}, bf16[16,128,1024]{2,1,0:T(8,128)(2,1)}, s32[16,128,32]{2,1,0:T(8,128)S(1)}, f32[16,128,32]{2,1,0:T(8,128)S(1)}, s32[]{:T(128)}) %tuple.44), condition=%wide.region_5.6_spmd.clone, body=%wide.region_3.5_spmd.clone.sunk | while | flops 12451842 | bytes 885317 | solution.py:36
  16.7 3.7 %select_reduce_fusion.4 = bf16[128,1024]{1,0:T(8,128)(2,1)S(1)} fusion(f32[128,32]{1,0:T(8,128)S(1)} %dynamic-slice_bitcast_fusion.4, s32[128,32]{1,0:T(8,128)S(1)} %dynamic-slice_bitcast_fusion.5), kind=kLoop, calls=%fused_computation.2.clone.1 | loop fusion | flops 12451840 | bytes 294912 | tf_op jit(solution)/shard_map/while/body/eval_jaxpr/reduce_sum | solution.py:34
  21.1 3.7 %select_reduce_fusion.4 = bf16[128,1024]{1,0:T(8,128)(2,1)S(1)} fusion(f32[128,32]{1,0:T(8,128)S(1)} %dynamic-slice_bitcast_fusion.4, s32[128,32]{1,0:T(8,128)S(1)} %dynamic-slice_bitcast_fusion.5), kind=kLoop, calls=%fused_computation.2.clone.1 | loop fusion | flops 12451840 | bytes 294912 | tf_op jit(solution)/shard_map/while/body/eval_jaxpr/reduce_sum | solution.py:34
  25.6 3.7 %select_reduce_fusion.4 = bf16[128,1024]{1,0:T(8,128)(2,1)S(1)} fusion(f32[128,32]{1,0:T(8,128)S(1)} %dynamic-slice_bitcast_fusion.4, s32[128,32]{1,0:T(8,128)S(1)} %dynamic-slice_bitcast_fusion.5), kind=kLoop, calls=%fused_computation.2.clone.1 | loop fusion | flops 12451840 | bytes 294912 | tf_op jit(solution)/shard_map/while/body/eval_jaxpr/reduce_sum | solution.py:34
  30.0 3.7 %select_reduce_fusion.4 = bf16[128,1024]{1,0:T(8,128)(2,1)S(1)} fusion(f32[128,32]{1,0:T(8,128)S(1)} %dynamic-slice_bitcast_fusion.4, s32[128,32]{1,0:T(8,128)S(1)} %dynamic-slice_bitcast_fusion.5), kind=kLoop, calls=%fused_computation.2.clone.1 | loop fusion | flops 12451840 | bytes 294912 | tf_op jit(solution)/shard_map/while/body/eval_jaxpr/reduce_sum | solution.py:34
  34.5 3.7 %select_reduce_fusion.4 = bf16[128,1024]{1,0:T(8,128)(2,1)S(1)} fusion(f32[128,32]{1,0:T(8,128)S(1)} %dynamic-slice_bitcast_fusion.4, s32[128,32]{1,0:T(8,128)S(1)} %dynamic-slice_bitcast_fusion.5), kind=kLoop, calls=%fused_computation.2.clone.1 | loop fusion | flops 12451840 | bytes 294912 | tf_op jit(solution)/shard_map/while/body/eval_jaxpr/reduce_sum | solution.py:34
  39.0 3.7 %select_reduce_fusion.4 = bf16[128,1024]{1,0:T(8,128)(2,1)S(1)} fusion(f32[128,32]{1,0:T(8,128)S(1)} %dynamic-slice_bitcast_fusion.4, s32[128,32]{1,0:T(8,128)S(1)} %dynamic-slice_bitcast_fusion.5), kind=kLoop, calls=%fused_computation.2.clone.1 | loop fusion | flops 12451840 | bytes 294912 | tf_op jit(solution)/shard_map/while/body/eval_jaxpr/reduce_sum | solution.py:34
  43.4 3.7 %select_reduce_fusion.4 = bf16[128,1024]{1,0:T(8,128)(2,1)S(1)} fusion(f32[128,32]{1,0:T(8,128)S(1)} %dynamic-slice_bitcast_fusion.4, s32[128,32]{1,0:T(8,128)S(1)} %dynamic-slice_bitcast_fusion.5), kind=kLoop, calls=%fused_computation.2.clone.1 | loop fusion | flops 12451840 | bytes 294912 | tf_op jit(solution)/shard_map/while/body/eval_jaxpr/reduce_sum | solution.py:34
  47.9 3.7 %select_reduce_fusion.4 = bf16[128,1024]{1,0:T(8,128)(2,1)S(1)} fusion(f32[128,32]{1,0:T(8,128)S(1)} %dynamic-slice_bitcast_fusion.4, s32[128,32]{1,0:T(8,128)S(1)} %dynamic-slice_bitcast_fusion.5), kind=kLoop, calls=%fused_computation.2.clone.1 | loop fusion | flops 12451840 | bytes 294912 | tf_op jit(solution)/shard_map/while/body/eval_jaxpr/reduce_sum | solution.py:34
  52.4 3.7 %select_reduce_fusion.4 = bf16[128,1024]{1,0:T(8,128)(2,1)S(1)} fusion(f32[128,32]{1,0:T(8,128)S(1)} %dynamic-slice_bitcast_fusion.4, s32[128,32]{1,0:T(8,128)S(1)} %dynamic-slice_bitcast_fusion.5), kind=kLoop, calls=%fused_computation.2.clone.1 | loop fusion | flops 12451840 | bytes 294912 | tf_op jit(solution)/shard_map/while/body/eval_jaxpr/reduce_sum | solution.py:34
  56.8 3.7 %select_reduce_fusion.4 = bf16[128,1024]{1,0:T(8,128)(2,1)S(1)} fusion(f32[128,32]{1,0:T(8,128)S(1)} %dynamic-slice_bitcast_fusion.4, s32[128,32]{1,0:T(8,128)S(1)} %dynamic-slice_bitcast_fusion.5), kind=kLoop, calls=%fused_computation.2.clone.1 | loop fusion | flops 12451840 | bytes 294912 | tf_op jit(solution)/shard_map/while/body/eval_jaxpr/reduce_sum | solution.py:34
  61.3 3.7 %select_reduce_fusion.4 = bf16[128,1024]{1,0:T(8,128)(2,1)S(1)} fusion(f32[128,32]{1,0:T(8,128)S(1)} %dynamic-slice_bitcast_fusion.4, s32[128,32]{1,0:T(8,128)S(1)} %dynamic-slice_bitcast_fusion.5), kind=kLoop, calls=%fused_computation.2.clone.1 | loop fusion | flops 12451840 | bytes 294912 | tf_op jit(solution)/shard_map/while/body/eval_jaxpr/reduce_sum | solution.py:34
  65.7 3.7 %select_reduce_fusion.4 = bf16[128,1024]{1,0:T(8,128)(2,1)S(1)} fusion(f32[128,32]{1,0:T(8,128)S(1)} %dynamic-slice_bitcast_fusion.4, s32[128,32]{1,0:T(8,128)S(1)} %dynamic-slice_bitcast_fusion.5), kind=kLoop, calls=%fused_computation.2.clone.1 | loop fusion | flops 12451840 | bytes 294912 | tf_op jit(solution)/shard_map/while/body/eval_jaxpr/reduce_sum | solution.py:34
  74.7 3.7 %select_reduce_fusion.4 = bf16[128,1024]{1,0:T(8,128)(2,1)S(1)} fusion(f32[128,32]{1,0:T(8,128)S(1)} %dynamic-slice_bitcast_fusion.4, s32[128,32]{1,0:T(8,128)S(1)} %dynamic-slice_bitcast_fusion.5), kind=kLoop, calls=%fused_computation.2.clone.1 | loop fusion | flops 12451840 | bytes 294912 | tf_op jit(solution)/shard_map/while/body/eval_jaxpr/reduce_sum | solution.py:34
  79.1 3.7 %select_reduce_fusion.4 = bf16[128,1024]{1,0:T(8,128)(2,1)S(1)} fusion(f32[128,32]{1,0:T(8,128)S(1)} %dynamic-slice_bitcast_fusion.4, s32[128,32]{1,0:T(8,128)S(1)} %dynamic-slice_bitcast_fusion.5), kind=kLoop, calls=%fused_computation.2.clone.1 | loop fusion | flops 12451840 | bytes 294912 | tf_op jit(solution)/shard_map/while/body/eval_jaxpr/reduce_sum | solution.py:34
  83.6 3.7 %select_reduce_fusion.4 = bf16[128,1024]{1,0:T(8,128)(2,1)S(1)} fusion(f32[128,32]{1,0:T(8,128)S(1)} %dynamic-slice_bitcast_fusion.4, s32[128,32]{1,0:T(8,128)S(1)} %dynamic-slice_bitcast_fusion.5), kind=kLoop, calls=%fused_computation.2.clone.1 | loop fusion | flops 12451840 | bytes 294912 | tf_op jit(solution)/shard_map/while/body/eval_jaxpr/reduce_sum | solution.py:34
  88.0 7.2 %reshape.35 = bf16[256,4,2,1024]{3,2,1,0:T(2,128)(2,1)} reshape(bf16[16,128,1024]{2,1,0:T(8,128)(2,1)} %get-tuple-element.29) | data formatting | bytes 8388608 | tf_op jit(solution)/shard_map/reshape | solution.py:36
  95.2 10.7 %fusion.6 = f32[1024,4,2,256]{3,0,2,1:T(8,128)} fusion(bf16[256,4,2,1024]{3,2,1,0:T(2,128)(2,1)} %reshape.35, bf16[256,4,2,256]{3,2,1,0:T(2,128)(2,1)S(1)} %copy-done), kind=kOutput, calls=%fused_computation.14 | convolution fusion | flops 1073741824 | bytes 13631488 | tf_op jit(solution)/shard_map/thxr,thxf->rhxf/dot_general | solution.py:46
  106.2 6.4 %fusion.9 = bf16[4,2,256,256]{2,3,1,0:T(8,128)(2,1)S(1)} fusion(bf16[1024,4,2,256]{0,3,2,1:T(8,128)(2,1)} %all-gather.2.cloned.1.call-done, bf16[256,4,2,1024]{3,2,1,0:T(2,128)(2,1)} %reshape.35), kind=kOutput, calls=%fused_computation.15 | convolution fusion | flops 1074266112 | bytes 9437184 | tf_op jit(solution)/shard_map/thxr,rhxf->thxf/dot_general | solution.py:38
  112.6 10.9 %fusion.22 = f32[256,4096]{1,0:T(8,128)} fusion(bf16[256,2048]{0,1:T(8,128)(2,1)S(1)} %bitcast.28, bf16[4096,2048]{1,0:T(8,128)(2,1)} %param.11), kind=kOutput, calls=%fused_computation.34 | convolution fusion | flops 4294967296 | bytes 22020096 | tf_op jit(solution)/shard_map/dot_general | solution.py:55
  123.5 71.5 %reduce-scatter.4.cloned.1.call-done = f32[256,4,2,256]{3,0,2,1:T(8,128)} async-done(((f32[1024,4,2,256]{3,0,2,1:T(8,128)}), f32[256,4,2,256]{3,0,2,1:T(8,128)}) %reduce-scatter.4.cloned.1.call-update) | async-done | bytes 2097168 | tf_op jit(solution)/shard_map/reduce_scatter | solution.py:45
  195.0 14.0 %reduce-scatter.8.cloned.1.call-done = f32[128,4096]{1,0:T(8,128)} async-done(((f32[256,4096]{1,0:T(8,128)}), f32[128,4096]{1,0:T(8,128)}) %reduce-scatter.8.cloned.1.call-update) | async-done | bytes 2097168 | tf_op jit(solution)/shard_map/reduce_scatter | solution.py:54
  211.8 44.5 %reduce-scatter.6.cloned.1.call-done = f32[64,4,2,256]{3,0,2,1:T(8,128)} async-done(((f32[256,4,2,256]{3,0,2,1:T(8,128)}), f32[64,4,2,256]{3,0,2,1:T(8,128)}) %reduce-scatter.6.cloned.1.call-update) | async-done | bytes 524304 | tf_op jit(solution)/shard_map/reduce_scatter | solution.py:51
  (71 shorter events, 25.7 us)
Async XLA Ops:
  8.0 87.2 %copy-start = (bf16[256,4,2,256]{3,2,1,0:T(2,128)(2,1)S(1)}, bf16[256,4,2,256]{3,2,1,0:T(2,128)(2,1)}, u32[]{:S(2)}) copy-start(bf16[256,4,2,256]{3,2,1,0:T(2,128)(2,1)} %param.9) | copy-start | bytes 3145732
  8.0 7.9 %copy-start.1 = (s32[256,4,2,32]{0,3,2,1:T(8,128)S(1)}, s32[256,4,2,32]{0,3,2,1:T(8,128)}, u32[]{:S(2)}) copy-start(s32[256,4,2,32]{0,3,2,1:T(8,128)} %param.12) | copy-start | bytes 786436
  8.0 98.2 %all-gather.2.cloned.1.call-start = ((), (), s32[]{:S(2)}) async-start(), calls=%async_computation.5 | async-start | bytes 5242880 | tf_op jit(solution)/shard_map/all_gather | solution.py:41
  11.8 183.2 %reduce-scatter.4.cloned.1.call-start = ((), (), s32[]{:S(2)}) async-start(), calls=%async_computation.3 | async-start | bytes 10485760 | tf_op jit(solution)/shard_map/reduce_scatter | solution.py:45
  105.9 103.1 %reduce-scatter.8.cloned.1.call-start = ((), (), s32[]{:S(2)}) async-start(), calls=%async_computation.6 | async-start | bytes 6291456 | tf_op jit(solution)/shard_map/reduce_scatter | solution.py:54
  123.5 132.8 %reduce-scatter.6.cloned.1.call-start = ((), (), s32[]{:S(2)}) async-start(), calls=%async_computation.4 | async-start | bytes 2621440 | tf_op jit(solution)/shard_map/reduce_scatter | solution.py:51
Sparse Core Ops, SparseCore 0:
  12.0 83.2 all-gather.1
Sparse Core Ops, SparseCore 1:
  106.0 88.9 reduce-scatter.3
  197.2 11.9 reduce-scatter.7
  211.2 44.9 reduce-scatter.5
where the time goes:
time: 267 us; the launch traced here: 266 us
  waiting for transfers between devices  130 us (49%)
  other arithmetic  65.2 us (24%)
  matrix products  27.9 us (10%)
  local copies, waits for them, and re-layouts  26.6 us (10%)
  between operations  15.7 us (6%)
    reduce_scatter x1, waiting for transfers between devices, on_device(): lax.psum_scatter(jnp.einsum('thxr,thxf->rhxf', part_rows, queries, prefer...  71.5 us
    reduce_sum x16, other arithmetic, build_rows(): jnp.sum(jnp.where(match, val_here[:, :, None], 0.0), axis=1)  59.3 us
    reduce_scatter x1, waiting for transfers between devices, on_device(): lax.psum_scatter(partial_value, 'key', scatter_dimension=0, tiled=True)  44.5 us
    reduce_scatter x1, waiting for transfers between devices, on_device(): lax.psum_scatter(lax.dot_general(part_rows, query_weight, (((1,), (1,)),...  14 us
    dynamic_update_slice x16, local copies, waits for them, and re-layouts, on_device(): lax.map(build_rows, (idx_blocks, val_blocks))  11.7 us
    dot_general x1, matrix products, on_device(): lax.dot_general(part_rows, query_weight, (((1,), (1,)), ((), ())), prefer...  10.9 us
    dot_general x1, matrix products, on_device(): jnp.einsum('thxr,thxf->rhxf', part_rows, queries, preferred_element_type=...  10.7 us
    reshape x1, local copies, waits for them, and re-layouts, on_device(): lax.map(build_rows, (idx_blocks, val_blocks))  7.2 us
  transfers between devices with their start and end apart: 4, of which 3 were waited for; matrix products, arithmetic and copies ran while one was open for 43% of the time, Pallas kernels for 0%

commit v1 on v0

v1 whole, which is shorter than its diff:
```python
import functools
import math

import jax
import jax.numpy as jnp
from jax import lax
from jax.experimental import pallas as pl
from jax.experimental.pallas import tpu as pltpu
from jax.sharding import PartitionSpec as P


F32 = jnp.float32
BF16 = jnp.bfloat16
VMEM_LIMIT = 24 * 1024 * 1024


def whole(memory_space=pltpu.VMEM):
    return pl.BlockSpec(memory_space=memory_space)


def row_code(rows):
    return (((rows & 127) + 128) << (rows >> 7)).astype(F32)


def prep_kernel(groups, per, topk, *refs):
    away, refs = refs[:4], refs[4:]
    outs, refs = refs[:groups], refs[groups:]
    here, sems = refs[:4], refs[4]
    copies = [pltpu.make_async_copy(a, b, sems.at[i]) for i, (a, b) in enumerate(zip(away, here))]
    for copy in copies:
        copy.start()
    for copy in copies:
        copy.wait()
    pair_ref, w_ref, wg_ref, sub_ref = here
    mine = lax.rem(lax.axis_index("dp"), groups)
    tok = pair_ref.shape[-1]
    slots = lax.broadcasted_iota(jnp.int32, (topk, tok), 0)
    for d in range(groups):
        for p in range(per):
            h = (mine ^ d) * per + p
            w = w_ref[h]
            wg = wg_ref[h]
            score = w * (wg - jnp.sum(w * wg, axis=0, keepdims=True))
            pairs = pair_ref[h]
            for x in range(2):
                slot = pairs // topk if x == 0 else pairs % topk
                grad = jnp.zeros((topk, tok), F32)
                for n in range(topk):
                    grad = grad + jnp.where(slot[n : n + 1] == slots, score[n : n + 1], 0.0)
                outs[d][p, x, 0] = row_code(sub_ref[h, x]).astype(BF16)
                outs[d][p, x, 1] = grad.astype(BF16)


def table_kernel(groups, per, topk, *refs):
    tabs, refs = refs[:groups], refs[groups:]
    table, code, value, names = refs
    nsub, wide = table.shape[1:]
    tok = wide // groups
    lanes, tile = 128, 16
    high = math.gcd(512, nsub)
    names[...] = row_code(lax.broadcasted_iota(jnp.int32, (nsub, lanes), 0))
    for p in range(per):
        for x in range(2):
            u = p * 2 + x
            for d in range(groups):
                code[:, d * tok : (d + 1) * tok] = tabs[d][p, x, 0].astype(F32)
                value[:, d * tok : (d + 1) * tok] = tabs[d][p, x, 1].astype(F32)

            def build(b, carry):
                row0 = lax.rem(b, nsub // high) * high
                lane0 = pl.multiple_of(lax.div(b, nsub // high) * lanes, lanes)
                rows = [pl.ds(pl.multiple_of(row0 + m * tile, tile), tile) for m in range(high // tile)]
                name = [names[r, :].astype(BF16) for r in rows]
                acc = [jnp.zeros((tile, lanes), BF16)] * len(rows)
                for s in range(topk):
                    c = jnp.broadcast_to(code[s : s + 1, pl.ds(lane0, lanes)], (tile, lanes)).astype(BF16)
                    v = jnp.broadcast_to(value[s : s + 1, pl.ds(lane0, lanes)], (tile, lanes)).astype(BF16)
                    acc = [jnp.where(n == c, v, a) for n, a in zip(name, acc)]
                for r, a in zip(rows, acc):
                    table[u, r, pl.ds(lane0, lanes)] = a
                return carry

            lax.fori_loop(0, (nsub // high) * (wide // lanes), build, 0)


def mix_kernel(groups, nkey, per, *refs):
    table, refs = refs[0], refs[1:]
    qs, refs = refs[:groups], refs[groups:]
    parts, total = refs[:nkey], refs[nkey]
    k = lax.axis_index("key")
    nsub = table.shape[1]
    tok, width = qs[0].shape[2:]
    blk = total.shape[1]
    high = min(256, nsub)
    for u in range(per * 2):
        for r in range(nsub // high):
            rows = slice(r * high, (r + 1) * high)
            acc = jnp.zeros((high, width), F32)
            for d in range(groups):
                acc = acc + jnp.dot(
                    table[u, rows, d * tok : (d + 1) * tok], qs[d][u // 2, u % 2], preferred_element_type=F32
                )
            per_blk = high // blk
            total[r * per_blk : (r + 1) * per_blk] = acc.reshape(per_blk, blk, width)
        for e in range(nkey):
            for m in range(parts[e].shape[1]):
                parts[e][u, m] = total[m * nkey + (k ^ e)].astype(parts[e].dtype)


def back_kernel(groups, nkey, per, *refs):
    table, refs = refs[0], refs[1:]
    ks, qgs = refs[:nkey], refs[nkey:]
    k = lax.axis_index("key")
    part = ks[0].shape[2]
    width, tok = qgs[0].shape[2:]
    for u in range(per * 2):
        p, x = u // 2, u % 2
        turned = [ks[e][p, x].T for e in range(nkey)]
        for d in range(groups):
            acc = jnp.zeros((width, tok), F32)
            for e in range(nkey):
                off = pl.multiple_of((k ^ e) * part, part)
                acc = acc + jnp.dot(
                    turned[e],
                    table[u, pl.ds(off, part), d * tok : (d + 1) * tok],
                    preferred_element_type=F32,
                )
            qgs[d][p, x] = acc.astype(BF16)


def sum_kernel(groups, nkey, *refs):
    ins, outs = refs[:nkey], refs[nkey:]
    mine = lax.rem(lax.axis_index("dp"), groups)
    for d in range(groups):
        acc = ins[0][:, mine ^ d]
        for e in range(1, nkey):
            acc = acc + ins[e][:, mine ^ d].astype(F32)
        outs[d][...] = acc.astype(outs[d].dtype)


def out_kernel(groups, ntensor, per, *refs):
    qgs, refs = refs[:groups], refs[groups:]
    w_ref, refs = refs[0], refs[1:]
    outs, right = refs[:ntensor], refs[ntensor]
    width, tok = qgs[0].shape[2:]
    here = tok // ntensor

    @pl.when(pl.program_id(0) == 0)
    def _():
        mine = lax.rem(lax.axis_index("dp"), groups)
        for d in range(groups):
            for p in range(per):
                for x in range(2):
                    u = ((mine ^ d) * per + p) * 2 + x
                    right[pl.ds(pl.multiple_of(u * width, width), width), :] = qgs[d][p, x]

    c = lax.axis_index("tensor")
    acc = jnp.dot(w_ref[...], right[...], preferred_element_type=F32)
    pieces = [acc[:, e * here : (e + 1) * here] for e in range(ntensor)]
    for e in range(ntensor):
        piece = pieces[0]
        for j in range(1, ntensor):
            piece = jnp.where((c ^ e) == j, pieces[j], piece)
        outs[e][...] = piece.astype(outs[e].dtype)


def join_kernel(*refs):
    acc = refs[0][...]
    for r in refs[1:-1]:
        acc = acc + r[...].astype(F32)
    refs[-1][...] = acc.T.astype(refs[-1].dtype)


def swap(x, axis, size, d):
    return lax.ppermute(x, axis, [(i, i ^ d) for i in range(size)])


def on_device(queries, sub_keys, query_weight, sub_choice, pair_choice, weights, weight_grad):
    tok, heads, halves, width = queries.shape
    topk = pair_choice.shape[2]
    ndp, nkey, ntensor = (lax.axis_size(a) for a in ("dp", "key", "tensor"))
    part = sub_keys.shape[0]
    nsub = part * nkey
    groups = math.gcd(ndp, heads)
    per = heads // groups
    rest = ndp // groups
    blk = nsub // (ndp * nkey)
    units = per * halves
    mine = lax.rem(lax.axis_index("dp"), groups)
    params = pltpu.CompilerParams(vmem_limit_bytes=VMEM_LIMIT)

    def of_heads(array, first):
        return jnp.transpose(lax.dynamic_slice_in_dim(array, first * per, per, 1), (1, 2, 0, 3))

    raw = (
        jnp.transpose(pair_choice, (1, 2, 0)),
        jnp.transpose(weights, (1, 2, 0)),
        jnp.transpose(weight_grad, (1, 2, 0)),
        jnp.transpose(sub_choice, (1, 2, 3, 0)),
    )
    tabs = pl.pallas_call(
        functools.partial(prep_kernel, groups, per, topk),
        out_shape=[jax.ShapeDtypeStruct((per, halves, 2, topk, tok), BF16)] * groups,
        in_specs=[whole(pltpu.HBM)] * 4,
        out_specs=[whole()] * groups,
        scratch_shapes=[pltpu.VMEM(r.shape, r.dtype) for r in raw] + [pltpu.SemaphoreType.DMA((4,))],
        compiler_params=params,
        name="prep",
    )(*[pltpu.with_memory_space_constraint(r, pltpu.HBM) for r in raw])
    own_keys = of_heads(sub_keys, mine)
    keys = [own_keys] + [swap(own_keys, "key", nkey, e) for e in range(1, nkey)]
    tabs = [tabs[0]] + [swap(tabs[d], "dp", ndp, d) for d in range(1, groups)]
    qs = [of_heads(queries, mine ^ d) for d in range(groups)]
    qs = [qs[0]] + [swap(qs[d], "dp", ndp, d) for d in range(1, groups)]

    table = pl.pallas_call(
        functools.partial(table_kernel, groups, per, topk),
        out_shape=jax.ShapeDtypeStruct((units, nsub, groups * tok), BF16),
        in_specs=[whole()] * groups,
        out_specs=whole(),
        scratch_shapes=[
            pltpu.VMEM((topk, groups * tok), F32),
            pltpu.VMEM((topk, groups * tok), F32),
            pltpu.VMEM((nsub, 128), F32),
        ],
        compiler_params=params,
        name="table",
    )(*tabs)
    parts = pl.pallas_call(
        functools.partial(mix_kernel, groups, nkey, per),
        out_shape=[
            jax.ShapeDtypeStruct((units, ndp, blk, width), F32 if e == 0 else BF16) for e in range(nkey)
        ],
        in_specs=[whole()] * (1 + groups),
        out_specs=[whole()] * nkey,
        scratch_shapes=[pltpu.VMEM((ndp * nkey, blk, width), F32)],
        compiler_params=params,
        name="mix",
    )(table, *qs)
    qgs = pl.pallas_call(
        functools.partial(back_kernel, groups, nkey, per),
        out_shape=[jax.ShapeDtypeStruct((per, halves, width, tok), BF16)] * groups,
        in_specs=[whole()] * (1 + nkey),
        out_specs=[whole()] * groups,
        compiler_params=params,
        name="back",
    )(table, *keys)
    parts = [parts[0]] + [swap(parts[e], "key", nkey, e) for e in range(1, nkey)]
    qgs = [qgs[0]] + [swap(qgs[d], "dp", ndp, d) for d in range(1, groups)]

    if rest > 1:
        summed = parts[0]
        for e in range(1, nkey):
            summed = summed + parts[e].astype(F32)
        summed = lax.psum_scatter(
            summed.reshape(units, rest, groups, blk, width),
            "dp",
            scatter_dimension=1,
            axis_index_groups=[[r * groups + g for r in range(rest)] for g in range(groups)],
            tiled=True,
        ).reshape(units, groups, blk, width)
        parts = [summed]
    pieces = pl.pallas_call(
        functools.partial(sum_kernel, groups, len(parts)),
        out_shape=[jax.ShapeDtypeStruct((units, blk, width), F32 if d == 0 else BF16) for d in range(groups)],
        in_specs=[whole()] * len(parts),
        out_specs=[whole()] * groups,
        compiler_params=params,
        name="sum",
    )(*parts)
    pieces = [pieces[0]] + [swap(pieces[d], "dp", ndp, d).astype(F32) for d in range(1, groups)]
    stacked = jnp.stack(pieces).reshape(groups, per, halves, blk, width)
    order = jnp.stack([lax.dynamic_index_in_dim(stacked, mine ^ d, 0, False) for d in range(groups)])
    sub_key_grad = jnp.transpose(order, (3, 0, 1, 2, 4)).reshape(blk, heads, halves, width)

    rows = query_weight.shape[0]
    bn = math.gcd(rows, 512)
    here = tok // ntensor
    outs = pl.pallas_call(
        functools.partial(out_kernel, groups, ntensor, per),
        out_shape=[jax.ShapeDtypeStruct((rows, here), F32 if e == 0 else BF16) for e in range(ntensor)],
        grid=(rows // bn,),
        in_specs=[pl.BlockSpec((per, halves, width, tok), lambda i: (0, 0, 0, 0))] * groups
        + [pl.BlockSpec((bn, heads * halves * width), lambda i: (i, 0))],
        out_specs=[pl.BlockSpec((bn, here), lambda i: (i, 0))] * ntensor,
        scratch_shapes=[pltpu.VMEM((heads * halves * width, tok), BF16)],
        compiler_params=params,
        name="out",
    )(*qgs, query_weight)
    outs = [outs[0]] + [swap(outs[e], "tensor", ntensor, e) for e in range(1, ntensor)]
    input_grad = pl.pallas_call(
        join_kernel,
        out_shape=jax.ShapeDtypeStruct((here, rows), BF16),
        in_specs=[whole()] * ntensor,
        out_specs=whole(),
        compiler_params=params,
        name="join",
    )(*outs)
    return sub_key_grad, input_grad


def solution(mesh):
    in_specs = (
        P(("dp", "key"), "tensor", None, None),
        P("key", "tensor", None, None),
        P(None, "tensor"),
        P(("dp", "key"), "tensor", None, None),
        P(("dp", "key"), "tensor", None),
        P(("dp", "key"), "tensor", None),
        P(("dp", "key"), "tensor", None),
    )
    out_specs = (P(("dp", "key"), "tensor", None, None), P(("dp", "key", "tensor"), None))

    return jax.shard_map(on_device, mesh=mesh, in_specs=in_specs, out_specs=out_specs, check_vma=False)
```

time: 267 us -> 83.6 us (0.31)
  the two profiles are of different devices: /device:TPU:0 before, /device:TPU:9 now
where the time goes in v1:
time: 83.6 us; the launch traced here: 83.5 us
  waiting for transfers between devices  36 us (43%)
  Pallas kernels  22.4 us (27%)
  starting transfers between devices  20.5 us (25%)
  local copies, waits for them, and re-layouts  3.58 us (4%)
  between operations  0.86 us (1%)
    ppermute x19, waiting for transfers between devices, swap(): return lax.ppermute(x, axis, [(i, i ^ d) for i in range(size)])  36 us
    ppermute x19, starting transfers between devices, swap(): return lax.ppermute(x, axis, [(i, i ^ d) for i in range(size)])  20.5 us
    pallas_call x1, Pallas kernels, on_device(): pl.pallas_call(functools.partial(table_kernel, groups, per, topk), out_sh...  9.93 us
    pallas_call x1, Pallas kernels, on_device(): pl.pallas_call(functools.partial(out_kernel, groups, ntensor, per), out_s...  5.91 us
    pallas_call x1, Pallas kernels, on_device(): pl.pallas_call(functools.partial(prep_kernel, groups, per, topk), out_sha...  2.48 us
    dynamic_slice x2, local copies, waits for them, and re-layouts, of_heads(): lax.dynamic_slice_in_dim(array, first * per, per, 1)  2.18 us
  transfers between devices with their start and end apart: 19, of which 6 were waited for; matrix products, arithmetic and copies ran while one was open for 2% of the time, Pallas kernels for 25%

profile of v1, /device:TPU:9, one launch (start us, length us, event | category | flops | bytes accessed | tf_op | source)
XLA Modules:
  0.0 83.5 jit_solution(12886528738671685570)
XLA Ops:
  0.7 2.0 %constant_dynamic-slice_fusion.1 = (bf16[256,1,2,256]{3,2,1,0:T(2,128)(2,1)S(1)}, bf16[256,1,2,256]{3,2,1,0:T(2,128)(2,1)S(1)}, bf16[256,1,2,256]{3,2,1,0:T(2,128)(2,1)S(1)}, bf16[256,1,2,256]{3,2,1,0:T(2,128)(2,1)S(1)}) fusion(bf16[256,4,2,256]{3,2,1,0:T(2,128)(2,1)} %param.7, s32[]{:T(128)S(6)} %select_n.21, s32[]{:T(128)S(6)} %select_n.20, ...), kind=kLoop, calls=%fused_computation.15 | loop fusion | bytes 2097168 | tf_op jit(solution)/shard_map/dynamic_slice | solution.py:193
  2.7 1.3 %collective-permute-start.3 = (bf16[1,2,256,256]{3,2,1,0:T(8,128)(2,1)S(1)}, bf16[1,2,256,256]{3,2,1,0:T(8,128)(2,1)S(1)}, u32[]{:S(2)}, u32[]{:S(2)}) collective-permute-start(bf16[1,2,256,256]{3,2,1,0:T(8,128)(2,1)S(1)} %bitcast.49), channel_id=1, source_target_pairs={{0,8},{8,0},{16,24},{24,16},{1,9},{9,1},{17,25},{25,17},{2,10},{10... | collective-permute-start | bytes 786440 | tf_op jit(solution)/shard_map/ppermute | solution.py:175
  4.0 1.3 %collective-permute-start.4 = (bf16[1,2,256,256]{3,2,1,0:T(8,128)(2,1)S(1)}, bf16[1,2,256,256]{3,2,1,0:T(8,128)(2,1)S(1)}, u32[]{:S(2)}, u32[]{:S(2)}) collective-permute-start(bf16[1,2,256,256]{3,2,1,0:T(8,128)(2,1)S(1)} %bitcast.48), channel_id=1, source_target_pairs={{0,16},{8,24},{16,0},{24,8},{1,17},{9,25},{17,1},{25,9},{2,18},{10... | collective-permute-start | bytes 786440 | tf_op jit(solution)/shard_map/ppermute | solution.py:175
  5.6 2.5 %prep.1 = (bf16[1,2,2,32,256]{4,3,2,1,0:T(8,128)(2,1)S(1)}, bf16[1,2,2,32,256]{4,3,2,1,0:T(8,128)(2,1)S(1)}, bf16[1,2,2,32,256]{4,3,2,1,0:T(8,128)(2,1)S(1)}, bf16[1,2,2,32,256]{4,3,2,1,0:T(8,128)(2,1)S(1)}) custom-call(s32[4,32,256]{2,1,0:T(8,128)} %bitcast.51, f32[4,32,256]{2,1,0:T(8,128)} %bitcast.52, f32[4,32,256]{2,1,0:T(8,128)} %bitcast.53, ...), custom_call_target="tpu_custom_call" | custom-call | tf_op jit(solution)/shard_map/prep/pallas_call | solution.py:201
  8.1 1.3 %collective-permute-start = (bf16[1,2,2,32,256]{4,3,2,1,0:T(8,128)(2,1)S(1)}, bf16[1,2,2,32,256]{4,3,2,1,0:T(8,128)(2,1)S(1)}, u32[]{:S(2)}, u32[]{:S(2)}) collective-permute-start(bf16[1,2,2,32,256]{4,3,2,1,0:T(8,128)(2,1)S(1)} %get-tuple-element.21), channel_id=1, source_target_pairs={{0,8},{8,0},{16,24},{24,16},{1,9},{9,1},{17,25},{25,17},{2,10},{10... | collective-permute-start | bytes 196616 | tf_op jit(solution)/shard_map/ppermute | solution.py:175
  9.4 1.2 %collective-permute-start.1 = (bf16[1,2,2,32,256]{4,3,2,1,0:T(8,128)(2,1)S(1)}, bf16[1,2,2,32,256]{4,3,2,1,0:T(8,128)(2,1)S(1)}, u32[]{:S(2)}, u32[]{:S(2)}) collective-permute-start(bf16[1,2,2,32,256]{4,3,2,1,0:T(8,128)(2,1)S(1)} %get-tuple-element.22), channel_id=1, source_target_pairs={{0,16},{8,24},{16,0},{24,8},{1,17},{9,25},{17,1},{25,9},{2,18},{10... | collective-permute-start | bytes 196616 | tf_op jit(solution)/shard_map/ppermute | solution.py:175
  10.6 6.4 %collective-permute-done.refs_1_ = bf16[1,2,2,32,256]{4,3,2,1,0:T(8,128)(2,1)S(1)} collective-permute-done((bf16[1,2,2,32,256]{4,3,2,1,0:T(8,128)(2,1)S(1)}, bf16[1,2,2,32,256]{4,3,2,1,0:T(8,128)(2,1)S(1)}, u32[]{:S(2)}, u32[]{:S(2)}) %collective-permute-start) | collective-permute-done | bytes 65568 | tf_op jit(solution)/shard_map/ppermute | solution.py:175
  17.0 2.2 %collective-permute-start.2 = (bf16[1,2,2,32,256]{4,3,2,1,0:T(8,128)(2,1)S(1)}, bf16[1,2,2,32,256]{4,3,2,1,0:T(8,128)(2,1)S(1)}, u32[]{:S(2)}, u32[]{:S(2)}) collective-permute-start(bf16[1,2,2,32,256]{4,3,2,1,0:T(8,128)(2,1)S(1)} %get-tuple-element.23), channel_id=1, source_target_pairs={{0,24},{8,16},{16,8},{24,0},{1,25},{9,17},{17,9},{25,1},{2,26},{10... | collective-permute-start | bytes 196616 | tf_op jit(solution)/shard_map/ppermute | solution.py:175
  19.7 1.3 %collective-permute-done.2.refs_3_ = bf16[1,2,2,32,256]{4,3,2,1,0:T(8,128)(2,1)S(1)} collective-permute-done((bf16[1,2,2,32,256]{4,3,2,1,0:T(8,128)(2,1)S(1)}, bf16[1,2,2,32,256]{4,3,2,1,0:T(8,128)(2,1)S(1)}, u32[]{:S(2)}, u32[]{:S(2)}) %collective-permute-start.2) | collective-permute-done | bytes 65568 | tf_op jit(solution)/shard_map/ppermute | solution.py:175
  21.0 2.3 %collective-permute-start.13 = (bf16[1,2,256,256]{3,2,1,0:T(8,128)(2,1)S(1)}, bf16[1,2,256,256]{3,2,1,0:T(8,128)(2,1)S(1)}, u32[]{:S(2)}, u32[]{:S(2)}) collective-permute-start(bf16[1,2,256,256]{3,2,1,0:T(8,128)(2,1)S(1)} %bitcast.42), channel_id=1, source_target_pairs={{0,4},{2,6},{4,0},{6,2},{1,5},{3,7},{5,1},{7,3},{8,12},{10,14},{12... | collective-permute-start | bytes 786440 | tf_op jit(solution)/shard_map/ppermute | solution.py:175
  23.4 9.9 %table.1.refs_0_ = bf16[2,1024,1024]{2,1,0:T(8,128)(2,1)S(1)} custom-call(bf16[1,2,2,32,256]{4,3,2,1,0:T(8,128)(2,1)S(1)} %get-tuple-element.20.refs_0_, bf16[1,2,2,32,256]{4,3,2,1,0:T(8,128)(2,1)S(1)} %collective-permute-done.refs_1_, bf16[1,2,2,32,256]{4,3,2,1,0:T(8,128)(2,1)S(1)} %collective-permute-done.1.refs_2_, ...), custom_call_target="tpu_custom_call" | custom-call | tf_op jit(solution)/shard_map/table/pallas_call | solution.py:216
  33.4 1.4 %mix.1 = (f32[2,4,64,256]{3,2,1,0:T(8,128)S(1)}, bf16[2,4,64,256]{3,2,1,0:T(8,128)(2,1)S(1)}, bf16[2,4,64,256]{3,2,1,0:T(8,128)(2,1)S(1)}, bf16[2,4,64,256]{3,2,1,0:T(8,128)(2,1)S(1)}) custom-call(bf16[2,1024,1024]{2,1,0:T(8,128)(2,1)S(1)} %table.1.refs_0_, bf16[1,2,256,256]{3,2,1,0:T(8,128)(2,1)S(1)} %bitcast.45, ...), custom_call_target="tpu_custom_call" | custom-call | tf_op jit(solution)/shard_map/mix/pallas_call | solution.py:229
  34.8 1.3 %collective-permute-start.6 = (bf16[2,4,64,256]{3,2,1,0:T(8,128)(2,1)S(1)}, bf16[2,4,64,256]{3,2,1,0:T(8,128)(2,1)S(1)}, u32[]{:S(2)}, u32[]{:S(2)}) collective-permute-start(bf16[2,4,64,256]{3,2,1,0:T(8,128)(2,1)S(1)} %get-tuple-element.25), channel_id=1, source_target_pairs={{0,2},{2,0},{4,6},{6,4},{1,3},{3,1},{5,7},{7,5},{8,10},{10,8},{12,... | collective-permute-start | bytes 786440 | tf_op jit(solution)/shard_map/ppermute | solution.py:175
  36.0 1.4 %collective-permute-start.7 = (bf16[2,4,64,256]{3,2,1,0:T(8,128)(2,1)S(1)}, bf16[2,4,64,256]{3,2,1,0:T(8,128)(2,1)S(1)}, u32[]{:S(2)}, u32[]{:S(2)}) collective-permute-start(bf16[2,4,64,256]{3,2,1,0:T(8,128)(2,1)S(1)} %get-tuple-element.26), channel_id=1, source_target_pairs={{0,4},{2,6},{4,0},{6,2},{1,5},{3,7},{5,1},{7,3},{8,12},{10,14},{12... | collective-permute-start | bytes 786440 | tf_op jit(solution)/shard_map/ppermute | solution.py:175
  37.5 10.5 %collective-permute-done.14.refs_4_ = bf16[1,2,256,256]{3,2,1,0:T(8,128)(2,1)S(1)} collective-permute-done((bf16[1,2,256,256]{3,2,1,0:T(8,128)(2,1)S(1)}, bf16[1,2,256,256]{3,2,1,0:T(8,128)(2,1)S(1)}, u32[]{:S(2)}, u32[]{:S(2)}) %collective-permute-start.14) | collective-permute-done | bytes 262176 | tf_op jit(solution)/shard_map/ppermute | solution.py:175
  47.9 1.3 %back.1 = (bf16[1,2,256,256]{3,2,1,0:T(8,128)(2,1)S(1)}, bf16[1,2,256,256]{3,2,1,0:T(8,128)(2,1)S(1)}, bf16[1,2,256,256]{3,2,1,0:T(8,128)(2,1)S(1)}, bf16[1,2,256,256]{3,2,1,0:T(8,128)(2,1)S(1)}) custom-call(bf16[2,1024,1024]{2,1,0:T(8,128)(2,1)S(1)} %table.1.refs_0_, bf16[1,2,256,256]{3,2,1,0:T(8,128)(2,1)S(1)} %bitcast.44, ...), custom_call_target="tpu_custom_call" | custom-call | tf_op jit(solution)/shard_map/back/pallas_call | solution.py:240
  49.2 1.3 %collective-permute-start.15 = (bf16[1,2,256,256]{3,2,1,0:T(8,128)(2,1)S(1)}, bf16[1,2,256,256]{3,2,1,0:T(8,128)(2,1)S(1)}, u32[]{:S(2)}, u32[]{:S(2)}) collective-permute-start(bf16[1,2,256,256]{3,2,1,0:T(8,128)(2,1)S(1)} %get-tuple-element.33), channel_id=1, source_target_pairs={{0,8},{8,0},{16,24},{24,16},{1,9},{9,1},{17,25},{25,17},{2,10},{10... | collective-permute-start | bytes 786440 | tf_op jit(solution)/shard_map/ppermute | solution.py:175
  50.5 1.2 %collective-permute-start.16 = (bf16[1,2,256,256]{3,2,1,0:T(8,128)(2,1)S(1)}, bf16[1,2,256,256]{3,2,1,0:T(8,128)(2,1)S(1)}, u32[]{:S(2)}, u32[]{:S(2)}) collective-permute-start(bf16[1,2,256,256]{3,2,1,0:T(8,128)(2,1)S(1)} %get-tuple-element.34), channel_id=1, source_target_pairs={{0,16},{8,24},{16,0},{24,8},{1,17},{9,25},{17,1},{25,9},{2,18},{10... | collective-permute-start | bytes 786440 | tf_op jit(solution)/shard_map/ppermute | solution.py:175
  51.9 10.0 %collective-permute-done.7.refs_2_ = bf16[2,4,64,256]{3,2,1,0:T(8,128)(2,1)S(1)} collective-permute-done((bf16[2,4,64,256]{3,2,1,0:T(8,128)(2,1)S(1)}, bf16[2,4,64,256]{3,2,1,0:T(8,128)(2,1)S(1)}, u32[]{:S(2)}, u32[]{:S(2)}) %collective-permute-start.7) | collective-permute-done | bytes 262176 | tf_op jit(solution)/shard_map/ppermute | solution.py:175
  62.0 6.9 %collective-permute-done.8.refs_3_ = bf16[2,4,64,256]{3,2,1,0:T(8,128)(2,1)S(1)} collective-permute-done((bf16[2,4,64,256]{3,2,1,0:T(8,128)(2,1)S(1)}, bf16[2,4,64,256]{3,2,1,0:T(8,128)(2,1)S(1)}, u32[]{:S(2)}, u32[]{:S(2)}) %collective-permute-start.8) | collective-permute-done | bytes 262176 | tf_op jit(solution)/shard_map/ppermute | solution.py:175
  69.0 2.2 %collective-permute-start.11 = (bf16[2,64,256]{2,1,0:T(8,128)(2,1)S(1)}, bf16[2,64,256]{2,1,0:T(8,128)(2,1)S(1)}, u32[]{:S(2)}, u32[]{:S(2)}) collective-permute-start(bf16[2,64,256]{2,1,0:T(8,128)(2,1)S(1)} %get-tuple-element.31), channel_id=1, source_target_pairs={{0,24},{8,16},{16,8},{24,0},{1,25},{9,17},{17,9},{25,1},{2,26},{10... | collective-permute-start | bytes 196616 | tf_op jit(solution)/shard_map/ppermute | solution.py:175
  71.7 5.9 %out.1 = (f32[4096,128]{1,0:T(8,128)S(1)}, bf16[4096,128]{1,0:T(8,128)(2,1)S(1)}) custom-call(bf16[1,2,256,256]{3,2,1,0:T(8,128)(2,1)S(1)} %get-tuple-element.32.refs_0_, bf16[1,2,256,256]{3,2,1,0:T(8,128)(2,1)S(1)} %collective-permute-done.15.refs_1_, bf16[1,2,256,256]{3,2,1,0:T(8,128)(2,1)S(1)} %collective-permute-done.16.refs_2_, ...), custom_call_target="tpu_custom_call" | custom-call | tf_op jit(solution)/shard_map/out/pallas_call | solution.py:279
  77.6 2.2 %collective-permute-start.18 = (bf16[4096,128]{1,0:T(8,128)(2,1)S(1)}, bf16[4096,128]{1,0:T(8,128)(2,1)S(1)}, u32[]{:S(2)}, u32[]{:S(2)}) collective-permute-start(bf16[4096,128]{1,0:T(8,128)(2,1)S(1)} %get-tuple-element.37), channel_id=1, source_target_pairs={{0,1},{1,0},{2,3},{3,2},{4,5},{5,4},{6,7},{7,6},{8,9},{9,8},{10,11... | collective-permute-start | bytes 3145736 | tf_op jit(solution)/shard_map/ppermute | solution.py:175
  82.1 1.3 %join.1 = bf16[128,4096]{1,0:T(8,128)(2,1)} custom-call(f32[4096,128]{1,0:T(8,128)S(1)} %get-tuple-element.36.refs_0_, bf16[4096,128]{1,0:T(8,128)(2,1)S(1)} %collective-permute-done.18.refs_1_), custom_call_target="tpu_custom_call" | custom-call | tf_op jit(solution)/shard_map/join/pallas_call | solution.py:291
  (39 shorter events, 4.0 us)
Async XLA Ops:
  0.6 18.6 %copy-start = (bf16[256,4,2,256]{3,2,1,0:T(2,128)(2,1)S(1)}, bf16[256,4,2,256]{3,2,1,0:T(2,128)(2,1)}, u32[]{:S(2)}) copy-start(bf16[256,4,2,256]{3,2,1,0:T(2,128)(2,1)} %param.8) | copy-start | bytes 3145732
  2.7 30.6 %collective-permute-start.3 = (bf16[1,2,256,256]{3,2,1,0:T(8,128)(2,1)S(1)}, bf16[1,2,256,256]{3,2,1,0:T(8,128)(2,1)S(1)}, u32[]{:S(2)}, u32[]{:S(2)}) collective-permute-start(bf16[1,2,256,256]{3,2,1,0:T(8,128)(2,1)S(1)} %bitcast.49), channel_id=1, source_target_pairs={{0,8},{8,0},{16,24},{24,16},{1,9},{9,1},{17,25},{25,17},{2,10},{10... | collective-permute-start | bytes 786440 | tf_op jit(solution)/shard_map/ppermute | solution.py:175
  4.0 29.4 %collective-permute-start.4 = (bf16[1,2,256,256]{3,2,1,0:T(8,128)(2,1)S(1)}, bf16[1,2,256,256]{3,2,1,0:T(8,128)(2,1)S(1)}, u32[]{:S(2)}, u32[]{:S(2)}) collective-permute-start(bf16[1,2,256,256]{3,2,1,0:T(8,128)(2,1)S(1)} %bitcast.48), channel_id=1, source_target_pairs={{0,16},{8,24},{16,0},{24,8},{1,17},{9,25},{17,1},{25,9},{2,18},{10... | collective-permute-start | bytes 786440 | tf_op jit(solution)/shard_map/ppermute | solution.py:175
  5.4 28.0 %collective-permute-start.5 = (bf16[1,2,256,256]{3,2,1,0:T(8,128)(2,1)S(1)}, bf16[1,2,256,256]{3,2,1,0:T(8,128)(2,1)S(1)}, u32[]{:S(2)}, u32[]{:S(2)}) collective-permute-start(bf16[1,2,256,256]{3,2,1,0:T(8,128)(2,1)S(1)} %bitcast.50), channel_id=1, source_target_pairs={{0,24},{8,16},{16,8},{24,0},{1,25},{9,17},{17,9},{25,1},{2,26},{10... | collective-permute-start | bytes 786440 | tf_op jit(solution)/shard_map/ppermute | solution.py:175
  8.1 8.9 %collective-permute-start = (bf16[1,2,2,32,256]{4,3,2,1,0:T(8,128)(2,1)S(1)}, bf16[1,2,2,32,256]{4,3,2,1,0:T(8,128)(2,1)S(1)}, u32[]{:S(2)}, u32[]{:S(2)}) collective-permute-start(bf16[1,2,2,32,256]{4,3,2,1,0:T(8,128)(2,1)S(1)} %get-tuple-element.21), channel_id=1, source_target_pairs={{0,8},{8,0},{16,24},{24,16},{1,9},{9,1},{17,25},{25,17},{2,10},{10... | collective-permute-start | bytes 196616 | tf_op jit(solution)/shard_map/ppermute | solution.py:175
  9.4 10.0 %collective-permute-start.1 = (bf16[1,2,2,32,256]{4,3,2,1,0:T(8,128)(2,1)S(1)}, bf16[1,2,2,32,256]{4,3,2,1,0:T(8,128)(2,1)S(1)}, u32[]{:S(2)}, u32[]{:S(2)}) collective-permute-start(bf16[1,2,2,32,256]{4,3,2,1,0:T(8,128)(2,1)S(1)} %get-tuple-element.22), channel_id=1, source_target_pairs={{0,16},{8,24},{16,0},{24,8},{1,17},{9,25},{17,1},{25,9},{2,18},{10... | collective-permute-start | bytes 196616 | tf_op jit(solution)/shard_map/ppermute | solution.py:175
  17.0 4.0 %collective-permute-start.2 = (bf16[1,2,2,32,256]{4,3,2,1,0:T(8,128)(2,1)S(1)}, bf16[1,2,2,32,256]{4,3,2,1,0:T(8,128)(2,1)S(1)}, u32[]{:S(2)}, u32[]{:S(2)}) collective-permute-start(bf16[1,2,2,32,256]{4,3,2,1,0:T(8,128)(2,1)S(1)} %get-tuple-element.23), channel_id=1, source_target_pairs={{0,24},{8,16},{16,8},{24,0},{1,25},{9,17},{17,9},{25,1},{2,26},{10... | collective-permute-start | bytes 196616 | tf_op jit(solution)/shard_map/ppermute | solution.py:175
  19.4 18.0 %collective-permute-start.12 = (bf16[1,2,256,256]{3,2,1,0:T(8,128)(2,1)S(1)}, bf16[1,2,256,256]{3,2,1,0:T(8,128)(2,1)S(1)}, u32[]{:S(2)}, u32[]{:S(2)}) collective-permute-start(bf16[1,2,256,256]{3,2,1,0:T(8,128)(2,1)S(1)} %bitcast.41), channel_id=1, source_target_pairs={{0,2},{2,0},{4,6},{6,4},{1,3},{3,1},{5,7},{7,5},{8,10},{10,8},{12,... | collective-permute-start | bytes 786440 | tf_op jit(solution)/shard_map/ppermute | solution.py:175
  19.7 52.0 %copy-start.1 = (bf16[4096,2048]{1,0:T(8,128)(2,1)S(1)}, bf16[4096,2048]{1,0:T(8,128)(2,1)}, u32[]{:S(2)}) copy-start(bf16[4096,2048]{1,0:T(8,128)(2,1)} %refs_4_.1) | copy-start | bytes 50331652
  21.0 16.4 %collective-permute-start.13 = (bf16[1,2,256,256]{3,2,1,0:T(8,128)(2,1)S(1)}, bf16[1,2,256,256]{3,2,1,0:T(8,128)(2,1)S(1)}, u32[]{:S(2)}, u32[]{:S(2)}) collective-permute-start(bf16[1,2,256,256]{3,2,1,0:T(8,128)(2,1)S(1)} %bitcast.42), channel_id=1, source_target_pairs={{0,4},{2,6},{4,0},{6,2},{1,5},{3,7},{5,1},{7,3},{8,12},{10,14},{12... | collective-permute-start | bytes 786440 | tf_op jit(solution)/shard_map/ppermute | solution.py:175
  33.3 14.6 %collective-permute-start.14 = (bf16[1,2,256,256]{3,2,1,0:T(8,128)(2,1)S(1)}, bf16[1,2,256,256]{3,2,1,0:T(8,128)(2,1)S(1)}, u32[]{:S(2)}, u32[]{:S(2)}) collective-permute-start(bf16[1,2,256,256]{3,2,1,0:T(8,128)(2,1)S(1)} %bitcast.43), channel_id=1, source_target_pairs={{0,6},{2,4},{4,2},{6,0},{1,7},{3,5},{5,3},{7,1},{8,14},{10,12},{12... | collective-permute-start | bytes 786440 | tf_op jit(solution)/shard_map/ppermute | solution.py:175
  34.8 17.0 %collective-permute-start.6 = (bf16[2,4,64,256]{3,2,1,0:T(8,128)(2,1)S(1)}, bf16[2,4,64,256]{3,2,1,0:T(8,128)(2,1)S(1)}, u32[]{:S(2)}, u32[]{:S(2)}) collective-permute-start(bf16[2,4,64,256]{3,2,1,0:T(8,128)(2,1)S(1)} %get-tuple-element.25), channel_id=1, source_target_pairs={{0,2},{2,0},{4,6},{6,4},{1,3},{3,1},{5,7},{7,5},{8,10},{10,8},{12,... | collective-permute-start | bytes 786440 | tf_op jit(solution)/shard_map/ppermute | solution.py:175
  36.0 25.9 %collective-permute-start.7 = (bf16[2,4,64,256]{3,2,1,0:T(8,128)(2,1)S(1)}, bf16[2,4,64,256]{3,2,1,0:T(8,128)(2,1)S(1)}, u32[]{:S(2)}, u32[]{:S(2)}) collective-permute-start(bf16[2,4,64,256]{3,2,1,0:T(8,128)(2,1)S(1)} %get-tuple-element.26), channel_id=1, source_target_pairs={{0,4},{2,6},{4,0},{6,2},{1,5},{3,7},{5,1},{7,3},{8,12},{10,14},{12... | collective-permute-start | bytes 786440 | tf_op jit(solution)/shard_map/ppermute | solution.py:175
  37.5 31.4 %collective-permute-start.8 = (bf16[2,4,64,256]{3,2,1,0:T(8,128)(2,1)S(1)}, bf16[2,4,64,256]{3,2,1,0:T(8,128)(2,1)S(1)}, u32[]{:S(2)}, u32[]{:S(2)}) collective-permute-start(bf16[2,4,64,256]{3,2,1,0:T(8,128)(2,1)S(1)} %get-tuple-element.27), channel_id=1, source_target_pairs={{0,6},{2,4},{4,2},{6,0},{1,7},{3,5},{5,3},{7,1},{8,14},{10,12},{12... | collective-permute-start | bytes 786440 | tf_op jit(solution)/shard_map/ppermute | solution.py:175
  49.2 22.2 %collective-permute-start.15 = (bf16[1,2,256,256]{3,2,1,0:T(8,128)(2,1)S(1)}, bf16[1,2,256,256]{3,2,1,0:T(8,128)(2,1)S(1)}, u32[]{:S(2)}, u32[]{:S(2)}) collective-permute-start(bf16[1,2,256,256]{3,2,1,0:T(8,128)(2,1)S(1)} %get-tuple-element.33), channel_id=1, source_target_pairs={{0,8},{8,0},{16,24},{24,16},{1,9},{9,1},{17,25},{25,17},{2,10},{10... | collective-permute-start | bytes 786440 | tf_op jit(solution)/shard_map/ppermute | solution.py:175
  50.5 21.2 %collective-permute-start.16 = (bf16[1,2,256,256]{3,2,1,0:T(8,128)(2,1)S(1)}, bf16[1,2,256,256]{3,2,1,0:T(8,128)(2,1)S(1)}, u32[]{:S(2)}, u32[]{:S(2)}) collective-permute-start(bf16[1,2,256,256]{3,2,1,0:T(8,128)(2,1)S(1)} %get-tuple-element.34), channel_id=1, source_target_pairs={{0,16},{8,24},{16,0},{24,8},{1,17},{9,25},{17,1},{25,9},{2,18},{10... | collective-permute-start | bytes 786440 | tf_op jit(solution)/shard_map/ppermute | solution.py:175
  51.7 20.0 %collective-permute-start.17 = (bf16[1,2,256,256]{3,2,1,0:T(8,128)(2,1)S(1)}, bf16[1,2,256,256]{3,2,1,0:T(8,128)(2,1)S(1)}, u32[]{:S(2)}, u32[]{:S(2)}) collective-permute-start(bf16[1,2,256,256]{3,2,1,0:T(8,128)(2,1)S(1)} %get-tuple-element.35), channel_id=1, source_target_pairs={{0,24},{8,16},{16,8},{24,0},{1,25},{9,17},{17,9},{25,1},{2,26},{10... | collective-permute-start | bytes 786440 | tf_op jit(solution)/shard_map/ppermute | solution.py:175
  69.0 10.9 %collective-permute-start.11 = (bf16[2,64,256]{2,1,0:T(8,128)(2,1)S(1)}, bf16[2,64,256]{2,1,0:T(8,128)(2,1)S(1)}, u32[]{:S(2)}, u32[]{:S(2)}) collective-permute-start(bf16[2,64,256]{2,1,0:T(8,128)(2,1)S(1)} %get-tuple-element.31), channel_id=1, source_target_pairs={{0,24},{8,16},{16,8},{24,0},{1,25},{9,17},{17,9},{25,1},{2,26},{10... | collective-permute-start | bytes 196616 | tf_op jit(solution)/shard_map/ppermute | solution.py:175
  71.2 8.7 %collective-permute-start.10 = (bf16[2,64,256]{2,1,0:T(8,128)(2,1)S(1)}, bf16[2,64,256]{2,1,0:T(8,128)(2,1)S(1)}, u32[]{:S(2)}, u32[]{:S(2)}) collective-permute-start(bf16[2,64,256]{2,1,0:T(8,128)(2,1)S(1)} %get-tuple-element.30), channel_id=1, source_target_pairs={{0,16},{8,24},{16,0},{24,8},{1,17},{9,25},{17,1},{25,9},{2,18},{10... | collective-permute-start | bytes 196616 | tf_op jit(solution)/shard_map/ppermute | solution.py:175
  71.4 8.5 %collective-permute-start.9 = (bf16[2,64,256]{2,1,0:T(8,128)(2,1)S(1)}, bf16[2,64,256]{2,1,0:T(8,128)(2,1)S(1)}, u32[]{:S(2)}, u32[]{:S(2)}) collective-permute-start(bf16[2,64,256]{2,1,0:T(8,128)(2,1)S(1)} %get-tuple-element.29), channel_id=1, source_target_pairs={{0,8},{8,0},{16,24},{24,16},{1,9},{9,1},{17,25},{25,17},{2,10},{10... | collective-permute-start | bytes 196616 | tf_op jit(solution)/shard_map/ppermute | solution.py:175
  77.6 4.5 %collective-permute-start.18 = (bf16[4096,128]{1,0:T(8,128)(2,1)S(1)}, bf16[4096,128]{1,0:T(8,128)(2,1)S(1)}, u32[]{:S(2)}, u32[]{:S(2)}) collective-permute-start(bf16[4096,128]{1,0:T(8,128)(2,1)S(1)} %get-tuple-element.37), channel_id=1, source_target_pairs={{0,1},{1,0},{2,3},{3,2},{4,5},{5,4},{6,7},{7,6},{8,9},{9,8},{10,11... | collective-permute-start | bytes 3145736 | tf_op jit(solution)/shard_map/ppermute | solution.py:175

commit v2 on v1

v2 whole, which is shorter than its diff:
```python
import functools
import math

import jax
import jax.numpy as jnp
from jax import lax
from jax.experimental import pallas as pl
from jax.experimental.pallas import tpu as pltpu
from jax.sharding import PartitionSpec as P


F32 = jnp.float32
BF16 = jnp.bfloat16
VMEM_LIMIT = 12 * 1024 * 1024


def whole(memory_space=pltpu.VMEM):
    return pl.BlockSpec(memory_space=memory_space)


def row_code(rows):
    return (((rows & 127) + 128) << (rows >> 7)).astype(F32)


def prep_kernel(groups, per, topk, *refs):
    away, refs = refs[:4], refs[4:]
    outs, refs = refs[:groups], refs[groups:]
    here, sems = refs[:4], refs[4]
    copies = [pltpu.make_async_copy(a, b, sems.at[i]) for i, (a, b) in enumerate(zip(away, here))]
    for copy in copies:
        copy.start()
    for copy in copies:
        copy.wait()
    pair_ref, w_ref, wg_ref, sub_ref = here
    mine = lax.rem(lax.axis_index("dp"), groups)
    tok = pair_ref.shape[-1]
    slots = lax.broadcasted_iota(jnp.int32, (topk, tok), 0)
    for d in range(groups):
        for p in range(per):
            h = (mine ^ d) * per + p
            w = w_ref[h]
            wg = wg_ref[h]
            score = w * (wg - jnp.sum(w * wg, axis=0, keepdims=True))
            pairs = pair_ref[h]
            for x in range(2):
                slot = pairs // topk if x == 0 else pairs % topk
                grad = jnp.zeros((topk, tok), F32)
                for n in range(topk):
                    grad = grad + jnp.where(slot[n : n + 1] == slots, score[n : n + 1], 0.0)
                outs[d][p, x, 0] = row_code(sub_ref[h, x]).astype(BF16)
                outs[d][p, x, 1] = grad.astype(BF16)


def table_kernel(units, topk, n, *refs):
    tabs, refs = refs[:n], refs[n:]
    tables, (code, value, names) = refs[: len(units)], refs[len(units) :]
    nsub, wide = tables[0].shape
    tok = wide // n
    lanes, tile = 128, 16
    high = math.gcd(512, nsub)
    names[...] = row_code(lax.broadcasted_iota(jnp.int32, (nsub, lanes), 0))
    for table, u in zip(tables, units):
        for d in range(n):
            code[:, d * tok : (d + 1) * tok] = tabs[d][u // 2, u % 2, 0].astype(F32)
            value[:, d * tok : (d + 1) * tok] = tabs[d][u // 2, u % 2, 1].astype(F32)

        def build(b, carry, table=table):
            row0 = lax.rem(b, nsub // high) * high
            lane0 = pl.multiple_of(lax.div(b, nsub // high) * lanes, lanes)
            rows = [pl.ds(pl.multiple_of(row0 + m * tile, tile), tile) for m in range(high // tile)]
            name = [names[r, :].astype(BF16) for r in rows]
            acc = [jnp.zeros((tile, lanes), BF16)] * len(rows)
            for s in range(topk):
                c = jnp.broadcast_to(code[s : s + 1, pl.ds(lane0, lanes)], (tile, lanes)).astype(BF16)
                v = jnp.broadcast_to(value[s : s + 1, pl.ds(lane0, lanes)], (tile, lanes)).astype(BF16)
                acc = [jnp.where(n == c, v, a) for n, a in zip(name, acc)]
            for r, a in zip(rows, acc):
                table[r, pl.ds(lane0, lanes)] = a
            return carry

        lax.fori_loop(0, (nsub // high) * (wide // lanes), build, 0)


def columns(d, tok):
    return slice(max(d - 1, 0) * tok, max(d - 1, 0) * tok + tok)


def mix_kernel(groups, keep_of, send_of, p, x, *refs):
    tables, refs = refs[: min(groups, 2)], refs[min(groups, 2) :]
    qs, refs = refs[:groups], refs[groups:]
    keep, send, total = refs
    k = lax.axis_index("key")
    nkey = len(keep_of) + len(send_of)
    nsub = tables[0].shape[0]
    tok, width = qs[0].shape[2:]
    blk = total.shape[1]
    high = min(256, nsub)
    for r in range(nsub // high):
        rows = slice(r * high, (r + 1) * high)
        acc = jnp.zeros((high, width), F32)
        for d in range(groups):
            acc = acc + jnp.dot(
                tables[min(d, 1)][rows, columns(d, tok)], qs[d][p, x], preferred_element_type=F32
            )
        per_blk = high // blk
        total[r * per_blk : (r + 1) * per_blk] = acc.reshape(per_blk, blk, width)
    for ref, which in ((keep, keep_of), (send, send_of)):
        for i, e in enumerate(which):
            for m in range(ref.shape[1]):
                ref[i, m] = total[m * nkey + (k ^ e)].astype(ref.dtype)


def halve_kernel(keep_at, send_at, kept, got, keep, send):
    for ref, which in ((keep, keep_at), (send, send_at)):
        for i, at in enumerate(which):
            ref[i] = (kept[at] + got[at].astype(F32)).astype(ref.dtype)


def back_kernel(groups, nkey, per, *refs):
    units = per * 2
    both = min(groups, 2)
    tables, refs = refs[: units * both], refs[units * both :]
    ks, qgs = refs[:nkey], refs[nkey:]
    k = lax.axis_index("key")
    part = ks[0].shape[2]
    width, tok = qgs[0].shape[2:]
    for u in range(units):
        p, x = u // 2, u % 2
        turned = [ks[e][p, x].T for e in range(nkey)]
        for d in range(groups):
            acc = jnp.zeros((width, tok), F32)
            for e in range(nkey):
                off = pl.multiple_of((k ^ e) * part, part)
                acc = acc + jnp.dot(
                    turned[e],
                    tables[u * both + min(d, 1)][pl.ds(off, part), columns(d, tok)],
                    preferred_element_type=F32,
                )
            qgs[d][p, x] = acc.astype(BF16)


def sum_kernel(groups, units, *refs):
    ins, outs = refs[:-groups], refs[-groups:]
    mine = lax.rem(lax.axis_index("dp"), groups)
    each = len(ins) // units
    for u in range(units):
        for d in range(groups):
            acc = ins[u * each][mine ^ d]
            for r in ins[u * each + 1 : (u + 1) * each]:
                acc = acc + r[mine ^ d].astype(F32)
            outs[d][u] = acc.astype(outs[d].dtype)


def first_kernel(groups, ds, per, *refs):
    qgs, (w_ref, out, right) = refs[: len(ds)], refs[len(ds) :]
    multiply(groups, ds, per, qgs, w_ref, right, out, None)


def second_kernel(groups, ds, ntensor, per, *refs):
    qgs, refs = refs[: len(ds)], refs[len(ds) :]
    w_ref, begun, refs = refs[0], refs[1], refs[2:]
    outs, right = refs[:ntensor], refs[ntensor]
    multiply(groups, ds, per, qgs, w_ref, right, outs, begun)


def multiply(groups, ds, per, qgs, w_ref, right, outs, begun):
    mine = lax.rem(lax.axis_index("dp"), groups)
    width, tok = qgs[0].shape[2:]
    span = per * 2 * width
    for i in range(len(ds)):
        for u in range(per * 2):
            right[i * span + u * width : i * span + (u + 1) * width, :] = qgs[i][u // 2, u % 2]
    offs = [pl.multiple_of((mine ^ d) * span, span) for d in ds]
    rows = w_ref.shape[0]
    high = math.gcd(rows, 512)

    def body(b, carry):
        at = pl.ds(pl.multiple_of(b * high, high), high)
        acc = jnp.zeros((high, tok), F32) if begun is None else begun[at, :]
        for i, off in enumerate(offs):
            acc = acc + jnp.dot(
                w_ref[at, pl.ds(off, span)], right[i * span : (i + 1) * span, :], preferred_element_type=F32
            )
        if begun is None:
            outs[at, :] = acc
            return carry
        n = len(outs)
        here = tok // n
        c = lax.axis_index("tensor")
        pieces = [acc[:, e * here : (e + 1) * here] for e in range(n)]
        for e in range(n):
            piece = pieces[0]
            for j in range(1, n):
                piece = jnp.where((c ^ e) == j, pieces[j], piece)
            outs[e][at, :] = piece.astype(outs[e].dtype)
        return carry

    lax.fori_loop(0, rows // high, body, 0)


def join_kernel(*refs):
    acc = refs[0][...]
    for r in refs[1:-1]:
        acc = acc + r[...].astype(F32)
    refs[-1][...] = acc.T.astype(refs[-1].dtype)


def swap(x, axis, size, d):
    return lax.ppermute(x, axis, [(i, i ^ d) for i in range(size)])


def on_device(queries, sub_keys, query_weight, sub_choice, pair_choice, weights, weight_grad):
    tok, heads, halves, width = queries.shape
    topk = pair_choice.shape[2]
    ndp, nkey, ntensor = (lax.axis_size(a) for a in ("dp", "key", "tensor"))
    part = sub_keys.shape[0]
    nsub = part * nkey
    groups = math.gcd(ndp, heads)
    per = heads // groups
    rest = ndp // groups
    blk = nsub // (ndp * nkey)
    units = per * halves
    mine = lax.rem(lax.axis_index("dp"), groups)
    params = pltpu.CompilerParams(vmem_limit_bytes=VMEM_LIMIT)

    def of_heads(array, first):
        return jnp.transpose(lax.dynamic_slice_in_dim(array, first * per, per, 1), (1, 2, 0, 3))

    raw = (
        jnp.transpose(pair_choice, (1, 2, 0)),
        jnp.transpose(weights, (1, 2, 0)),
        jnp.transpose(weight_grad, (1, 2, 0)),
        jnp.transpose(sub_choice, (1, 2, 3, 0)),
    )
    tabs = pl.pallas_call(
        functools.partial(prep_kernel, groups, per, topk),
        out_shape=[jax.ShapeDtypeStruct((per, halves, 2, topk, tok), BF16)] * groups,
        in_specs=[whole(pltpu.HBM)] * 4,
        out_specs=[whole()] * groups,
        scratch_shapes=[pltpu.VMEM(r.shape, r.dtype) for r in raw] + [pltpu.SemaphoreType.DMA((4,))],
        compiler_params=params,
        name="prep",
    )(*[pltpu.with_memory_space_constraint(r, pltpu.HBM) for r in raw])
    own_keys = of_heads(sub_keys, mine)
    keys = [own_keys] + [swap(own_keys, "key", nkey, e) for e in range(1, nkey)]
    tabs = [tabs[0]] + [swap(tabs[d], "dp", ndp, d) for d in range(1, groups)]
    qs = [of_heads(queries, mine ^ d) for d in range(groups)]
    qs = [qs[0]] + [swap(qs[d], "dp", ndp, d) for d in range(1, groups)]

    def call(kernel, outs, *ins, scratch=()):
        many = isinstance(outs, (list, tuple))
        return pl.pallas_call(
            kernel,
            out_shape=outs,
            in_specs=[whole()] * len(ins),
            out_specs=[whole()] * len(outs) if many else whole(),
            scratch_shapes=list(scratch),
            compiler_params=params,
        )(*ins)

    shape = jax.ShapeDtypeStruct
    left = list(range(nkey))
    keep_of = [e for e in left if not e & 1]
    send_of = [e for e in left if e & 1]
    tables, halves_of = [], []

    def build(which, sources):
        wide = len(sources) * tok
        return call(
            functools.partial(table_kernel, which, topk, len(sources)),
            [shape((nsub, wide), BF16)] * len(which),
            *sources,
            scratch=[
                pltpu.VMEM((topk, wide), F32),
                pltpu.VMEM((topk, wide), F32),
                pltpu.VMEM((nsub, 128), F32),
            ],
        )

    mine_tables = build(list(range(units)), tabs[:1])
    tabs = tabs[1:]
    for u in range(units):
        p, x = u // halves, u % halves
        table = [mine_tables[u]] + (list(build([u], tabs)) if tabs else [])
        keep, send = call(
            functools.partial(mix_kernel, groups, keep_of, send_of, p, x),
            [
                shape((len(keep_of), ndp, blk, width), F32),
                shape((len(send_of), ndp, blk, width), BF16),
            ],
            *table,
            *qs,
            scratch=[pltpu.VMEM((ndp * nkey, blk, width), F32)],
        )
        got = swap(send, "key", nkey, 1)
        tables += table
        halves_of.append((keep, got))
    qgs = call(
        functools.partial(back_kernel, groups, nkey, per),
        [shape((per, halves, width, tok), BF16)] * groups,
        *tables,
        *keys,
    )
    qgs = [qgs[0]] + [swap(qgs[d], "dp", ndp, d) for d in range(1, groups)]

    parts = []
    for keep, got in halves_of:
        left, bit = keep_of, 2
        while len(left) > 1:
            keep_at = [i for i, e in enumerate(left) if not e & bit]
            send_at = [i for i, e in enumerate(left) if e & bit]
            keep, send = call(
                functools.partial(halve_kernel, keep_at, send_at),
                [
                    shape((len(keep_at), ndp, blk, width), F32),
                    shape((len(send_at), ndp, blk, width), BF16),
                ],
                keep,
                got,
            )
            got = swap(send, "key", nkey, bit)
            left, bit = [left[i] for i in keep_at], bit * 2
        parts += [keep.reshape(ndp, blk, width), got.reshape(ndp, blk, width)]

    if rest > 1:
        summed = jnp.stack([parts[2 * u] + parts[2 * u + 1].astype(F32) for u in range(units)])
        summed = lax.psum_scatter(
            summed.reshape(units, rest, groups, blk, width),
            "dp",
            scatter_dimension=1,
            axis_index_groups=[[r * groups + g for r in range(rest)] for g in range(groups)],
            tiled=True,
        ).reshape(units, groups, blk, width)
        parts = [summed[u] for u in range(units)]
    pieces = call(
        functools.partial(sum_kernel, groups, units),
        [shape((units, blk, width), F32 if d == 0 else BF16) for d in range(groups)],
        *parts,
    )
    pieces = [pieces[0]] + [swap(pieces[d], "dp", ndp, d) for d in range(1, groups)]
    pieces = [p.astype(F32) for p in pieces]
    stacked = jnp.stack(pieces).reshape(groups, per, halves, blk, width)
    order = jnp.stack([lax.dynamic_index_in_dim(stacked, mine ^ d, 0, False) for d in range(groups)])
    sub_key_grad = jnp.transpose(order, (3, 0, 1, 2, 4)).reshape(blk, heads, halves, width)

    rows = query_weight.shape[0]
    here = tok // ntensor
    early = [0] if groups > 1 else []
    late = list(range(len(early), groups))
    span = per * halves * width
    if early:
        begun = call(
            functools.partial(first_kernel, groups, early, per),
            shape((rows, tok), F32),
            *[qgs[d] for d in early],
            query_weight,
            scratch=[pltpu.VMEM((len(early) * span, tok), BF16)],
        )
    else:
        begun = jnp.zeros((rows, tok), F32)
    outs = call(
        functools.partial(second_kernel, groups, late, ntensor, per),
        [shape((rows, here), F32 if e == 0 else BF16) for e in range(ntensor)],
        *[qgs[d] for d in late],
        query_weight,
        begun,
        scratch=[pltpu.VMEM((len(late) * span, tok), BF16)],
    )
    outs = [outs[0]] + [swap(outs[e], "tensor", ntensor, e) for e in range(1, ntensor)]
    input_grad = pl.pallas_call(
        join_kernel,
        out_shape=jax.ShapeDtypeStruct((here, rows), BF16),
        in_specs=[whole()] * ntensor,
        out_specs=whole(),
        compiler_params=params,
        name="join",
    )(*outs)
    return sub_key_grad, input_grad


def solution(mesh):
    in_specs = (
        P(("dp", "key"), "tensor", None, None),
        P("key", "tensor", None, None),
        P(None, "tensor"),
        P(("dp", "key"), "tensor", None, None),
        P(("dp", "key"), "tensor", None),
        P(("dp", "key"), "tensor", None),
        P(("dp", "key"), "tensor", None),
    )
    out_specs = (P(("dp", "key"), "tensor", None, None), P(("dp", "key", "tensor"), None))

    return jax.shard_map(
        on_device, mesh=mesh, in_specs=in_specs, out_specs=out_specs, check_vma=False
    )
```

time: 83.6 us -> 81 us (0.969)
  the two profiles are of different devices: /device:TPU:9 before, /device:TPU:0 now
where the time goes in v2:
time: 81 us; the launch traced here: 80.8 us
  starting transfers between devices  29.5 us (36%)
  Pallas kernels  24 us (30%)
  waiting for transfers between devices  22.7 us (28%)
  local copies, waits for them, and re-layouts  3.59 us (4%)
  between operations  0.92 us (1%)
    ppermute x20, starting transfers between devices, swap(): return lax.ppermute(x, axis, [(i, i ^ d) for i in range(size)])  29.5 us
    ppermute x20, waiting for transfers between devices, swap(): return lax.ppermute(x, axis, [(i, i ^ d) for i in range(size)])  22.7 us
    pallas_call x11, Pallas kernels, call(): pl.pallas_call(kernel, out_shape=outs, in_specs=[whole()] * len(ins), out...  20.2 us
    pallas_call x1, Pallas kernels, on_device(): pl.pallas_call(functools.partial(prep_kernel, groups, per, topk), out_sha...  2.49 us
    dynamic_slice x2, local copies, waits for them, and re-layouts, of_heads(): lax.dynamic_slice_in_dim(array, first * per, per, 1)  2.18 us
  transfers between devices with their start and end apart: 20, of which 6 were waited for; matrix products, arithmetic and copies ran while one was open for 2% of the time, Pallas kernels for 28%

profile of v2, /device:TPU:0, one launch (start us, length us, event | category | flops | bytes accessed | tf_op | source)
XLA Modules:
  0.0 80.8 jit_solution(1111532249849919932)
XLA Ops:
  0.7 2.0 %constant_dynamic-slice_fusion.1 = (bf16[256,1,2,256]{3,2,1,0:T(2,128)(2,1)S(1)}, bf16[256,1,2,256]{3,2,1,0:T(2,128)(2,1)S(1)}, bf16[256,1,2,256]{3,2,1,0:T(2,128)(2,1)S(1)}, bf16[256,1,2,256]{3,2,1,0:T(2,128)(2,1)S(1)}) fusion(bf16[256,4,2,256]{3,2,1,0:T(2,128)(2,1)} %param.7, s32[]{:T(128)S(6)} %select_n.21, s32[]{:T(128)S(6)} %select_n.20, ...), kind=kLoop, calls=%fused_computation.15 | loop fusion | bytes 2097168 | tf_op jit(solution)/shard_map/dynamic_slice | solution.py:227
  2.7 3.0 %collective-permute-start.3 = (bf16[1,2,256,256]{3,2,1,0:T(8,128)(2,1)S(1)}, bf16[1,2,256,256]{3,2,1,0:T(8,128)(2,1)S(1)}, u32[]{:S(2)}, u32[]{:S(2)}) collective-permute-start(bf16[1,2,256,256]{3,2,1,0:T(8,128)(2,1)S(1)} %bitcast.59), channel_id=1, source_target_pairs={{0,8},{8,0},{16,24},{24,16},{1,9},{9,1},{17,25},{25,17},{2,10},{10... | collective-permute-start | bytes 786440 | tf_op jit(solution)/shard_map/ppermute | solution.py:209
  5.8 1.6 %collective-permute-start.4 = (bf16[1,2,256,256]{3,2,1,0:T(8,128)(2,1)S(1)}, bf16[1,2,256,256]{3,2,1,0:T(8,128)(2,1)S(1)}, u32[]{:S(2)}, u32[]{:S(2)}) collective-permute-start(bf16[1,2,256,256]{3,2,1,0:T(8,128)(2,1)S(1)} %bitcast.57), channel_id=1, source_target_pairs={{0,16},{8,24},{16,0},{24,8},{1,17},{9,25},{17,1},{25,9},{2,18},{10... | collective-permute-start | bytes 786440 | tf_op jit(solution)/shard_map/ppermute | solution.py:209
  7.5 2.5 %prep.1 = (bf16[1,2,2,32,256]{4,3,2,1,0:T(8,128)(2,1)S(1)}, bf16[1,2,2,32,256]{4,3,2,1,0:T(8,128)(2,1)S(1)}, bf16[1,2,2,32,256]{4,3,2,1,0:T(8,128)(2,1)S(1)}, bf16[1,2,2,32,256]{4,3,2,1,0:T(8,128)(2,1)S(1)}) custom-call(s32[4,32,256]{2,1,0:T(8,128)} %bitcast.60, f32[4,32,256]{2,1,0:T(8,128)} %bitcast.61, f32[4,32,256]{2,1,0:T(8,128)} %bitcast.62, ...), custom_call_target="tpu_custom_call" | custom-call | tf_op jit(solution)/shard_map/prep/pallas_call | solution.py:235
  10.0 2.0 %collective-permute-start = (bf16[1,2,2,32,256]{4,3,2,1,0:T(8,128)(2,1)S(1)}, bf16[1,2,2,32,256]{4,3,2,1,0:T(8,128)(2,1)S(1)}, u32[]{:S(2)}, u32[]{:S(2)}) collective-permute-start(bf16[1,2,2,32,256]{4,3,2,1,0:T(8,128)(2,1)S(1)} %get-tuple-element.28), channel_id=1, source_target_pairs={{0,8},{8,0},{16,24},{24,16},{1,9},{9,1},{17,25},{25,17},{2,10},{10... | collective-permute-start | bytes 196616 | tf_op jit(solution)/shard_map/ppermute | solution.py:209
  12.0 1.5 %collective-permute-start.1 = (bf16[1,2,2,32,256]{4,3,2,1,0:T(8,128)(2,1)S(1)}, bf16[1,2,2,32,256]{4,3,2,1,0:T(8,128)(2,1)S(1)}, u32[]{:S(2)}, u32[]{:S(2)}) collective-permute-start(bf16[1,2,2,32,256]{4,3,2,1,0:T(8,128)(2,1)S(1)} %get-tuple-element.29), channel_id=1, source_target_pairs={{0,16},{8,24},{16,0},{24,8},{1,17},{9,25},{17,1},{25,9},{2,18},{10... | collective-permute-start | bytes 196616 | tf_op jit(solution)/shard_map/ppermute | solution.py:209
  13.5 5.6 %collective-permute-done.refs_0_ = bf16[1,2,2,32,256]{4,3,2,1,0:T(8,128)(2,1)S(1)} collective-permute-done((bf16[1,2,2,32,256]{4,3,2,1,0:T(8,128)(2,1)S(1)}, bf16[1,2,2,32,256]{4,3,2,1,0:T(8,128)(2,1)S(1)}, u32[]{:S(2)}, u32[]{:S(2)}) %collective-permute-start) | collective-permute-done | bytes 65568 | tf_op jit(solution)/shard_map/ppermute | solution.py:209
  19.1 2.7 %collective-permute-start.2 = (bf16[1,2,2,32,256]{4,3,2,1,0:T(8,128)(2,1)S(1)}, bf16[1,2,2,32,256]{4,3,2,1,0:T(8,128)(2,1)S(1)}, u32[]{:S(2)}, u32[]{:S(2)}) collective-permute-start(bf16[1,2,2,32,256]{4,3,2,1,0:T(8,128)(2,1)S(1)} %get-tuple-element.30), channel_id=1, source_target_pairs={{0,24},{8,16},{16,8},{24,0},{1,25},{9,17},{17,9},{25,1},{2,26},{10... | collective-permute-start | bytes 196616 | tf_op jit(solution)/shard_map/ppermute | solution.py:209
  22.0 3.7 %collective-permute-start.15 = (bf16[1,2,256,256]{3,2,1,0:T(8,128)(2,1)S(1)}, bf16[1,2,256,256]{3,2,1,0:T(8,128)(2,1)S(1)}, u32[]{:S(2)}, u32[]{:S(2)}) collective-permute-start(bf16[1,2,256,256]{3,2,1,0:T(8,128)(2,1)S(1)} %bitcast.47), channel_id=1, source_target_pairs={{0,6},{2,4},{4,2},{6,0},{1,7},{3,5},{5,3},{7,1},{8,14},{10,12},{12... | collective-permute-start | bytes 786440 | tf_op jit(solution)/shard_map/ppermute | solution.py:209
  27.1 1.6 %collective-permute-start.13 = (bf16[1,2,256,256]{3,2,1,0:T(8,128)(2,1)S(1)}, bf16[1,2,256,256]{3,2,1,0:T(8,128)(2,1)S(1)}, u32[]{:S(2)}, u32[]{:S(2)}) collective-permute-start(bf16[1,2,256,256]{3,2,1,0:T(8,128)(2,1)S(1)} %bitcast.49), channel_id=1, source_target_pairs={{0,2},{2,0},{4,6},{6,4},{1,3},{3,1},{5,7},{7,5},{8,10},{10,8},{12,... | collective-permute-start | bytes 786440 | tf_op jit(solution)/shard_map/ppermute | solution.py:209
  28.7 2.6 %shard_map.86 = (bf16[1024,256]{1,0:T(8,128)(2,1)S(1)}, bf16[1024,256]{1,0:T(8,128)(2,1)S(1)}) custom-call(bf16[1,2,2,32,256]{4,3,2,1,0:T(8,128)(2,1)S(1)} %get-tuple-element.26.refs_0_), custom_call_target="tpu_custom_call" | custom-call | tf_op jit(solution)/shard_map/pallas_call | solution.py:252
  31.3 3.8 %shard_map.90.refs_1_.refs_3_ = bf16[1024,768]{1,0:T(8,128)(2,1)S(1)} custom-call(bf16[1,2,2,32,256]{4,3,2,1,0:T(8,128)(2,1)S(1)} %collective-permute-done.refs_0_, bf16[1,2,2,32,256]{4,3,2,1,0:T(8,128)(2,1)S(1)} %collective-permute-done.1.refs_1_, bf16[1,2,2,32,256]{4,3,2,1,0:T(8,128)(2,1)S(1)} %collective-permute-done.2.refs_2_), custom_call_target="tpu_custom_call" | custom-call | tf_op jit(solution)/shard_map/pallas_call | solution.py:252
  36.4 3.8 %shard_map.87.refs_1_ = bf16[1024,768]{1,0:T(8,128)(2,1)S(1)} custom-call(bf16[1,2,2,32,256]{4,3,2,1,0:T(8,128)(2,1)S(1)} %collective-permute-done.refs_0_, bf16[1,2,2,32,256]{4,3,2,1,0:T(8,128)(2,1)S(1)} %collective-permute-done.1.refs_1_, bf16[1,2,2,32,256]{4,3,2,1,0:T(8,128)(2,1)S(1)} %collective-permute-done.2.refs_2_), custom_call_target="tpu_custom_call" | custom-call | tf_op jit(solution)/shard_map/pallas_call | solution.py:252
  41.0 1.6 %collective-permute-start.6 = (bf16[2,4,64,256]{3,2,1,0:T(8,128)(2,1)S(1)}, bf16[2,4,64,256]{3,2,1,0:T(8,128)(2,1)S(1)}, u32[]{:S(2)}, u32[]{:S(2)}) collective-permute-start(bf16[2,4,64,256]{3,2,1,0:T(8,128)(2,1)S(1)} %get-tuple-element.32), channel_id=1, source_target_pairs={{0,2},{2,0},{4,6},{6,4},{1,3},{3,1},{5,7},{7,5},{8,10},{10,8},{12,... | collective-permute-start | bytes 786440 | tf_op jit(solution)/shard_map/ppermute | solution.py:209
  42.6 4.3 %collective-permute-done.14.refs_6_ = bf16[1,2,256,256]{3,2,1,0:T(8,128)(2,1)S(1)} collective-permute-done((bf16[1,2,256,256]{3,2,1,0:T(8,128)(2,1)S(1)}, bf16[1,2,256,256]{3,2,1,0:T(8,128)(2,1)S(1)}, u32[]{:S(2)}, u32[]{:S(2)}) %collective-permute-start.14) | collective-permute-done | bytes 262176 | tf_op jit(solution)/shard_map/ppermute | solution.py:209
  49.4 2.4 %collective-permute-start.18 = (bf16[1,2,256,256]{3,2,1,0:T(8,128)(2,1)S(1)}, bf16[1,2,256,256]{3,2,1,0:T(8,128)(2,1)S(1)}, u32[]{:S(2)}, u32[]{:S(2)}) collective-permute-start(bf16[1,2,256,256]{3,2,1,0:T(8,128)(2,1)S(1)} %get-tuple-element.46), channel_id=1, source_target_pairs={{0,24},{8,16},{16,8},{24,0},{1,25},{9,17},{17,9},{25,1},{2,26},{10... | collective-permute-start | bytes 786440 | tf_op jit(solution)/shard_map/ppermute | solution.py:209
  52.0 2.1 %collective-permute-done.6.got = bf16[2,4,64,256]{3,2,1,0:T(8,128)(2,1)S(1)} collective-permute-done((bf16[2,4,64,256]{3,2,1,0:T(8,128)(2,1)S(1)}, bf16[2,4,64,256]{3,2,1,0:T(8,128)(2,1)S(1)}, u32[]{:S(2)}, u32[]{:S(2)}) %collective-permute-start.6) | collective-permute-done | bytes 262176 | tf_op jit(solution)/shard_map/ppermute | solution.py:209
  54.2 2.5 %collective-permute-start.7 = (bf16[1,4,64,256]{3,2,1,0:T(8,128)(2,1)S(1)}, bf16[1,4,64,256]{3,2,1,0:T(8,128)(2,1)S(1)}, u32[]{:S(2)}, u32[]{:S(2)}) collective-permute-start(bf16[1,4,64,256]{3,2,1,0:T(8,128)(2,1)S(1)} %get-tuple-element.34), channel_id=1, source_target_pairs={{0,4},{2,6},{4,0},{6,2},{1,5},{3,7},{5,1},{7,3},{8,12},{10,14},{12... | collective-permute-start | bytes 393224 | tf_op jit(solution)/shard_map/ppermute | solution.py:209
  56.6 6.3 %collective-permute-done.9 = bf16[1,4,64,256]{3,2,1,0:T(8,128)(2,1)S(1)} collective-permute-done((bf16[1,4,64,256]{3,2,1,0:T(8,128)(2,1)S(1)}, bf16[1,4,64,256]{3,2,1,0:T(8,128)(2,1)S(1)}, u32[]{:S(2)}, u32[]{:S(2)}) %collective-permute-start.9) | collective-permute-done | bytes 131104 | tf_op jit(solution)/shard_map/ppermute | solution.py:209
  62.9 1.4 %collective-permute-done.7 = bf16[1,4,64,256]{3,2,1,0:T(8,128)(2,1)S(1)} collective-permute-done((bf16[1,4,64,256]{3,2,1,0:T(8,128)(2,1)S(1)}, bf16[1,4,64,256]{3,2,1,0:T(8,128)(2,1)S(1)}, u32[]{:S(2)}, u32[]{:S(2)}) %collective-permute-start.7) | collective-permute-done | bytes 131104 | tf_op jit(solution)/shard_map/ppermute | solution.py:209
  65.0 2.4 %shard_map.95.refs_4_ = f32[4096,256]{1,0:T(8,128)S(1)} custom-call(bf16[1,2,256,256]{3,2,1,0:T(8,128)(2,1)S(1)} %get-tuple-element.47.refs_0_, bf16[4096,2048]{1,0:T(8,128)(2,1)S(1)} %copy-done.1), custom_call_target="tpu_custom_call" | custom-call | tf_op jit(solution)/shard_map/pallas_call | solution.py:252
  67.4 4.7 %shard_map.96 = (f32[4096,128]{1,0:T(8,128)S(1)}, bf16[4096,128]{1,0:T(8,128)(2,1)S(1)}) custom-call(bf16[1,2,256,256]{3,2,1,0:T(8,128)(2,1)S(1)} %collective-permute-done.16.refs_0_, bf16[1,2,256,256]{3,2,1,0:T(8,128)(2,1)S(1)} %collective-permute-done.17.refs_1_, bf16[1,2,256,256]{3,2,1,0:T(8,128)(2,1)S(1)} %collective-permute-done.18.refs_2_, ...), custom_call_target="tpu_custom_call" | custom-call | tf_op jit(solution)/shard_map/pallas_call | solution.py:252
  72.8 2.4 %collective-permute-start.12 = (bf16[2,64,256]{2,1,0:T(8,128)(2,1)S(1)}, bf16[2,64,256]{2,1,0:T(8,128)(2,1)S(1)}, u32[]{:S(2)}, u32[]{:S(2)}) collective-permute-start(bf16[2,64,256]{2,1,0:T(8,128)(2,1)S(1)} %get-tuple-element.43), channel_id=1, source_target_pairs={{0,24},{8,16},{16,8},{24,0},{1,25},{9,17},{17,9},{25,1},{2,26},{10... | collective-permute-start | bytes 196616 | tf_op jit(solution)/shard_map/ppermute | solution.py:209
  75.2 2.9 %collective-permute-done.11 = bf16[2,64,256]{2,1,0:T(8,128)(2,1)S(1)} collective-permute-done((bf16[2,64,256]{2,1,0:T(8,128)(2,1)S(1)}, bf16[2,64,256]{2,1,0:T(8,128)(2,1)S(1)}, u32[]{:S(2)}, u32[]{:S(2)}) %collective-permute-start.11) | collective-permute-done | bytes 65568 | tf_op jit(solution)/shard_map/ppermute | solution.py:209
  (47 shorter events, 10.5 us)
Async XLA Ops:
  0.6 21.2 %copy-start = (bf16[256,4,2,256]{3,2,1,0:T(2,128)(2,1)S(1)}, bf16[256,4,2,256]{3,2,1,0:T(2,128)(2,1)}, u32[]{:S(2)}) copy-start(bf16[256,4,2,256]{3,2,1,0:T(2,128)(2,1)} %param.8) | copy-start | bytes 3145732
  2.7 24.4 %collective-permute-start.3 = (bf16[1,2,256,256]{3,2,1,0:T(8,128)(2,1)S(1)}, bf16[1,2,256,256]{3,2,1,0:T(8,128)(2,1)S(1)}, u32[]{:S(2)}, u32[]{:S(2)}) collective-permute-start(bf16[1,2,256,256]{3,2,1,0:T(8,128)(2,1)S(1)} %bitcast.59), channel_id=1, source_target_pairs={{0,8},{8,0},{16,24},{24,16},{1,9},{9,1},{17,25},{25,17},{2,10},{10... | collective-permute-start | bytes 786440 | tf_op jit(solution)/shard_map/ppermute | solution.py:209
  5.8 29.3 %collective-permute-start.4 = (bf16[1,2,256,256]{3,2,1,0:T(8,128)(2,1)S(1)}, bf16[1,2,256,256]{3,2,1,0:T(8,128)(2,1)S(1)}, u32[]{:S(2)}, u32[]{:S(2)}) collective-permute-start(bf16[1,2,256,256]{3,2,1,0:T(8,128)(2,1)S(1)} %bitcast.57), channel_id=1, source_target_pairs={{0,16},{8,24},{16,0},{24,8},{1,17},{9,25},{17,1},{25,9},{2,18},{10... | collective-permute-start | bytes 786440 | tf_op jit(solution)/shard_map/ppermute | solution.py:209
  7.4 27.7 %collective-permute-start.5 = (bf16[1,2,256,256]{3,2,1,0:T(8,128)(2,1)S(1)}, bf16[1,2,256,256]{3,2,1,0:T(8,128)(2,1)S(1)}, u32[]{:S(2)}, u32[]{:S(2)}) collective-permute-start(bf16[1,2,256,256]{3,2,1,0:T(8,128)(2,1)S(1)} %bitcast.58), channel_id=1, source_target_pairs={{0,24},{8,16},{16,8},{24,0},{1,25},{9,17},{17,9},{25,1},{2,26},{10... | collective-permute-start | bytes 786440 | tf_op jit(solution)/shard_map/ppermute | solution.py:209
  10.0 9.1 %collective-permute-start = (bf16[1,2,2,32,256]{4,3,2,1,0:T(8,128)(2,1)S(1)}, bf16[1,2,2,32,256]{4,3,2,1,0:T(8,128)(2,1)S(1)}, u32[]{:S(2)}, u32[]{:S(2)}) collective-permute-start(bf16[1,2,2,32,256]{4,3,2,1,0:T(8,128)(2,1)S(1)} %get-tuple-element.28), channel_id=1, source_target_pairs={{0,8},{8,0},{16,24},{24,16},{1,9},{9,1},{17,25},{25,17},{2,10},{10... | collective-permute-start | bytes 196616 | tf_op jit(solution)/shard_map/ppermute | solution.py:209
  12.0 10.1 %collective-permute-start.1 = (bf16[1,2,2,32,256]{4,3,2,1,0:T(8,128)(2,1)S(1)}, bf16[1,2,2,32,256]{4,3,2,1,0:T(8,128)(2,1)S(1)}, u32[]{:S(2)}, u32[]{:S(2)}) collective-permute-start(bf16[1,2,2,32,256]{4,3,2,1,0:T(8,128)(2,1)S(1)} %get-tuple-element.29), channel_id=1, source_target_pairs={{0,16},{8,24},{16,0},{24,8},{1,17},{9,25},{17,1},{25,9},{2,18},{10... | collective-permute-start | bytes 196616 | tf_op jit(solution)/shard_map/ppermute | solution.py:209
  19.1 6.6 %collective-permute-start.2 = (bf16[1,2,2,32,256]{4,3,2,1,0:T(8,128)(2,1)S(1)}, bf16[1,2,2,32,256]{4,3,2,1,0:T(8,128)(2,1)S(1)}, u32[]{:S(2)}, u32[]{:S(2)}) collective-permute-start(bf16[1,2,2,32,256]{4,3,2,1,0:T(8,128)(2,1)S(1)} %get-tuple-element.30), channel_id=1, source_target_pairs={{0,24},{8,16},{16,8},{24,0},{1,25},{9,17},{17,9},{25,1},{2,26},{10... | collective-permute-start | bytes 196616 | tf_op jit(solution)/shard_map/ppermute | solution.py:209
  22.0 20.6 %collective-permute-start.15 = (bf16[1,2,256,256]{3,2,1,0:T(8,128)(2,1)S(1)}, bf16[1,2,256,256]{3,2,1,0:T(8,128)(2,1)S(1)}, u32[]{:S(2)}, u32[]{:S(2)}) collective-permute-start(bf16[1,2,256,256]{3,2,1,0:T(8,128)(2,1)S(1)} %bitcast.47), channel_id=1, source_target_pairs={{0,6},{2,4},{4,2},{6,0},{1,7},{3,5},{5,3},{7,1},{8,14},{10,12},{12... | collective-permute-start | bytes 786440 | tf_op jit(solution)/shard_map/ppermute | solution.py:209
  25.7 21.3 %collective-permute-start.14 = (bf16[1,2,256,256]{3,2,1,0:T(8,128)(2,1)S(1)}, bf16[1,2,256,256]{3,2,1,0:T(8,128)(2,1)S(1)}, u32[]{:S(2)}, u32[]{:S(2)}) collective-permute-start(bf16[1,2,256,256]{3,2,1,0:T(8,128)(2,1)S(1)} %bitcast.48), channel_id=1, source_target_pairs={{0,4},{2,6},{4,0},{6,2},{1,5},{3,7},{5,1},{7,3},{8,12},{10,14},{12... | collective-permute-start | bytes 786440 | tf_op jit(solution)/shard_map/ppermute | solution.py:209
  27.1 19.9 %collective-permute-start.13 = (bf16[1,2,256,256]{3,2,1,0:T(8,128)(2,1)S(1)}, bf16[1,2,256,256]{3,2,1,0:T(8,128)(2,1)S(1)}, u32[]{:S(2)}, u32[]{:S(2)}) collective-permute-start(bf16[1,2,256,256]{3,2,1,0:T(8,128)(2,1)S(1)} %bitcast.49), channel_id=1, source_target_pairs={{0,2},{2,0},{4,6},{6,4},{1,3},{3,1},{5,7},{7,5},{8,10},{10,8},{12,... | collective-permute-start | bytes 786440 | tf_op jit(solution)/shard_map/ppermute | solution.py:209
  31.3 33.7 %copy-start.1 = (bf16[4096,2048]{1,0:T(8,128)(2,1)S(1)}, bf16[4096,2048]{1,0:T(8,128)(2,1)}, u32[]{:S(2)}) copy-start(bf16[4096,2048]{1,0:T(8,128)(2,1)} %refs_3_.1) | copy-start | bytes 50331652
  35.9 15.9 %collective-permute-start.8 = (bf16[2,4,64,256]{3,2,1,0:T(8,128)(2,1)S(1)}, bf16[2,4,64,256]{3,2,1,0:T(8,128)(2,1)S(1)}, u32[]{:S(2)}, u32[]{:S(2)}) collective-permute-start(bf16[2,4,64,256]{3,2,1,0:T(8,128)(2,1)S(1)} %get-tuple-element.37), channel_id=1, source_target_pairs={{0,2},{2,0},{4,6},{6,4},{1,3},{3,1},{5,7},{7,5},{8,10},{10,8},{12,... | collective-permute-start | bytes 786440 | tf_op jit(solution)/shard_map/ppermute | solution.py:209
  41.0 13.1 %collective-permute-start.6 = (bf16[2,4,64,256]{3,2,1,0:T(8,128)(2,1)S(1)}, bf16[2,4,64,256]{3,2,1,0:T(8,128)(2,1)S(1)}, u32[]{:S(2)}, u32[]{:S(2)}) collective-permute-start(bf16[2,4,64,256]{3,2,1,0:T(8,128)(2,1)S(1)} %get-tuple-element.32), channel_id=1, source_target_pairs={{0,2},{2,0},{4,6},{6,4},{1,3},{3,1},{5,7},{7,5},{8,10},{10,8},{12,... | collective-permute-start | bytes 786440 | tf_op jit(solution)/shard_map/ppermute | solution.py:209
  48.3 19.1 %collective-permute-start.16 = (bf16[1,2,256,256]{3,2,1,0:T(8,128)(2,1)S(1)}, bf16[1,2,256,256]{3,2,1,0:T(8,128)(2,1)S(1)}, u32[]{:S(2)}, u32[]{:S(2)}) collective-permute-start(bf16[1,2,256,256]{3,2,1,0:T(8,128)(2,1)S(1)} %get-tuple-element.44), channel_id=1, source_target_pairs={{0,8},{8,0},{16,24},{24,16},{1,9},{9,1},{17,25},{25,17},{2,10},{10... | collective-permute-start | bytes 786440 | tf_op jit(solution)/shard_map/ppermute | solution.py:209
  48.9 18.5 %collective-permute-start.17 = (bf16[1,2,256,256]{3,2,1,0:T(8,128)(2,1)S(1)}, bf16[1,2,256,256]{3,2,1,0:T(8,128)(2,1)S(1)}, u32[]{:S(2)}, u32[]{:S(2)}) collective-permute-start(bf16[1,2,256,256]{3,2,1,0:T(8,128)(2,1)S(1)} %get-tuple-element.45), channel_id=1, source_target_pairs={{0,16},{8,24},{16,0},{24,8},{1,17},{9,25},{17,1},{25,9},{2,18},{10... | collective-permute-start | bytes 786440 | tf_op jit(solution)/shard_map/ppermute | solution.py:209
  49.4 18.0 %collective-permute-start.18 = (bf16[1,2,256,256]{3,2,1,0:T(8,128)(2,1)S(1)}, bf16[1,2,256,256]{3,2,1,0:T(8,128)(2,1)S(1)}, u32[]{:S(2)}, u32[]{:S(2)}) collective-permute-start(bf16[1,2,256,256]{3,2,1,0:T(8,128)(2,1)S(1)} %get-tuple-element.46), channel_id=1, source_target_pairs={{0,24},{8,16},{16,8},{24,0},{1,25},{9,17},{17,9},{25,1},{2,26},{10... | collective-permute-start | bytes 786440 | tf_op jit(solution)/shard_map/ppermute | solution.py:209
  51.9 11.0 %collective-permute-start.9 = (bf16[1,4,64,256]{3,2,1,0:T(8,128)(2,1)S(1)}, bf16[1,4,64,256]{3,2,1,0:T(8,128)(2,1)S(1)}, u32[]{:S(2)}, u32[]{:S(2)}) collective-permute-start(bf16[1,4,64,256]{3,2,1,0:T(8,128)(2,1)S(1)} %get-tuple-element.39), channel_id=1, source_target_pairs={{0,4},{2,6},{4,0},{6,2},{1,5},{3,7},{5,1},{7,3},{8,12},{10,14},{12... | collective-permute-start | bytes 393224 | tf_op jit(solution)/shard_map/ppermute | solution.py:209
  54.2 10.2 %collective-permute-start.7 = (bf16[1,4,64,256]{3,2,1,0:T(8,128)(2,1)S(1)}, bf16[1,4,64,256]{3,2,1,0:T(8,128)(2,1)S(1)}, u32[]{:S(2)}, u32[]{:S(2)}) collective-permute-start(bf16[1,4,64,256]{3,2,1,0:T(8,128)(2,1)S(1)} %get-tuple-element.34), channel_id=1, source_target_pairs={{0,4},{2,6},{4,0},{6,2},{1,5},{3,7},{5,1},{7,3},{8,12},{10,14},{12... | collective-permute-start | bytes 393224 | tf_op jit(solution)/shard_map/ppermute | solution.py:209
  64.4 10.8 %collective-permute-start.10 = (bf16[2,64,256]{2,1,0:T(8,128)(2,1)S(1)}, bf16[2,64,256]{2,1,0:T(8,128)(2,1)S(1)}, u32[]{:S(2)}, u32[]{:S(2)}) collective-permute-start(bf16[2,64,256]{2,1,0:T(8,128)(2,1)S(1)} %get-tuple-element.41), channel_id=1, source_target_pairs={{0,8},{8,0},{16,24},{24,16},{1,9},{9,1},{17,25},{25,17},{2,10},{10... | collective-permute-start | bytes 196616 | tf_op jit(solution)/shard_map/ppermute | solution.py:209
  72.1 7.4 %collective-permute-start.19 = (bf16[4096,128]{1,0:T(8,128)(2,1)S(1)}, bf16[4096,128]{1,0:T(8,128)(2,1)S(1)}, u32[]{:S(2)}, u32[]{:S(2)}) collective-permute-start(bf16[4096,128]{1,0:T(8,128)(2,1)S(1)} %get-tuple-element.49), channel_id=1, source_target_pairs={{0,1},{1,0},{2,3},{3,2},{4,5},{5,4},{6,7},{7,6},{8,9},{9,8},{10,11... | collective-permute-start | bytes 3145736 | tf_op jit(solution)/shard_map/ppermute | solution.py:209
  72.2 5.9 %collective-permute-start.11 = (bf16[2,64,256]{2,1,0:T(8,128)(2,1)S(1)}, bf16[2,64,256]{2,1,0:T(8,128)(2,1)S(1)}, u32[]{:S(2)}, u32[]{:S(2)}) collective-permute-start(bf16[2,64,256]{2,1,0:T(8,128)(2,1)S(1)} %get-tuple-element.42), channel_id=1, source_target_pairs={{0,16},{8,24},{16,0},{24,8},{1,17},{9,25},{17,1},{25,9},{2,18},{10... | collective-permute-start | bytes 196616 | tf_op jit(solution)/shard_map/ppermute | solution.py:209
  72.8 5.3 %collective-permute-start.12 = (bf16[2,64,256]{2,1,0:T(8,128)(2,1)S(1)}, bf16[2,64,256]{2,1,0:T(8,128)(2,1)S(1)}, u32[]{:S(2)}, u32[]{:S(2)}) collective-permute-start(bf16[2,64,256]{2,1,0:T(8,128)(2,1)S(1)} %get-tuple-element.43), channel_id=1, source_target_pairs={{0,24},{8,16},{16,8},{24,0},{1,25},{9,17},{17,9},{25,1},{2,26},{10... | collective-permute-start | bytes 196616 | tf_op jit(solution)/shard_map/ppermute | solution.py:209

commit v3 on v2

--- a/solution.py
+++ b/solution.py
@@ -23,16 +23,22 @@
 
 
 def prep_kernel(groups, per, topk, *refs):
-    away, refs = refs[:4], refs[4:]
-    outs, refs = refs[:groups], refs[groups:]
+    away, (q_ref, k_ref), refs = refs[:4], refs[4:6], refs[6:]
+    outs, cuts, refs = refs[:groups], refs[groups : 2 * groups + 1], refs[2 * groups + 1 :]
     here, sems = refs[:4], refs[4]
+    mine = lax.rem(lax.axis_index("dp"), groups)
     copies = [pltpu.make_async_copy(a, b, sems.at[i]) for i, (a, b) in enumerate(zip(away, here))]
-    for copy in copies:
+    later = [
+        pltpu.make_async_copy(k_ref.at[:, pl.ds(mine * per, per)], cuts[groups], sems.at[4])
+    ] + [
+        pltpu.make_async_copy(q_ref.at[:, pl.ds((mine ^ d) * per, per)], cuts[d], sems.at[5 + d])
+        for d in range(groups)
+    ]
+    for copy in copies + later:
         copy.start()
     for copy in copies:
         copy.wait()
     pair_ref, w_ref, wg_ref, sub_ref = here
-    mine = lax.rem(lax.axis_index("dp"), groups)
     tok = pair_ref.shape[-1]
     slots = lax.broadcasted_iota(jnp.int32, (topk, tok), 0)
     for d in range(groups):
@@ -49,6 +55,8 @@
                     grad = grad + jnp.where(slot[n : n + 1] == slots, score[n : n + 1], 0.0)
                 outs[d][p, x, 0] = row_code(sub_ref[h, x]).astype(BF16)
                 outs[d][p, x, 1] = grad.astype(BF16)
+    for copy in later:
+        copy.wait()
 
 
 def table_kernel(units, topk, n, *refs):
@@ -57,7 +65,7 @@
     nsub, wide = tables[0].shape
     tok = wide // n
     lanes, tile = 128, 16
-    high = math.gcd(512, nsub)
+    high = math.gcd(1024, nsub)
     names[...] = row_code(lax.broadcasted_iota(jnp.int32, (nsub, lanes), 0))
     for table, u in zip(tables, units):
         for d in range(n):
@@ -172,10 +180,10 @@
             right[i * span + u * width : i * span + (u + 1) * width, :] = qgs[i][u // 2, u % 2]
     offs = [pl.multiple_of((mine ^ d) * span, span) for d in ds]
     rows = w_ref.shape[0]
-    high = math.gcd(rows, 512)
-
-    def body(b, carry):
-        at = pl.ds(pl.multiple_of(b * high, high), high)
+    high = math.gcd(rows, 1024)
+
+    for b in range(rows // high):
+        at = slice(b * high, (b + 1) * high)
         acc = jnp.zeros((high, tok), F32) if begun is None else begun[at, :]
         for i, off in enumerate(offs):
             acc = acc + jnp.dot(
@@ -183,7 +191,7 @@
             )
         if begun is None:
             outs[at, :] = acc
-            return carry
+            continue
         n = len(outs)
         here = tok // n
         c = lax.axis_index("tensor")
@@ -193,9 +201,6 @@
             for j in range(1, n):
                 piece = jnp.where((c ^ e) == j, pieces[j], piece)
             outs[e][at, :] = piece.astype(outs[e].dtype)
-        return carry
-
-    lax.fori_loop(0, rows // high, body, 0)
 
 
 def join_kernel(*refs):
@@ -223,8 +228,8 @@
     mine = lax.rem(lax.axis_index("dp"), groups)
     params = pltpu.CompilerParams(vmem_limit_bytes=VMEM_LIMIT)
 
-    def of_heads(array, first):
-        return jnp.transpose(lax.dynamic_slice_in_dim(array, first * per, per, 1), (1, 2, 0, 3))
+    def by_head(cut):
+        return jnp.transpose(cut, (1, 2, 0, 3))
 
     raw = (
         jnp.transpose(pair_choice, (1, 2, 0)),
@@ -232,19 +237,22 @@
         jnp.transpose(weight_grad, (1, 2, 0)),
         jnp.transpose(sub_choice, (1, 2, 3, 0)),
     )
-    tabs = pl.pallas_call(
+    prepared = pl.pallas_call(
         functools.partial(prep_kernel, groups, per, topk),
-        out_shape=[jax.ShapeDtypeStruct((per, halves, 2, topk, tok), BF16)] * groups,
-        in_specs=[whole(pltpu.HBM)] * 4,
-        out_specs=[whole()] * groups,
-        scratch_shapes=[pltpu.VMEM(r.shape, r.dtype) for r in raw] + [pltpu.SemaphoreType.DMA((4,))],
+        out_shape=[jax.ShapeDtypeStruct((per, halves, 2, topk, tok), BF16)] * groups
+        + [jax.ShapeDtypeStruct((tok, per, halves, width), BF16)] * groups
+        + [jax.ShapeDtypeStruct((part, per, halves, width), BF16)],
+        in_specs=[whole(pltpu.HBM)] * 6,
+        out_specs=[whole()] * (2 * groups + 1),
+        scratch_shapes=[pltpu.VMEM(r.shape, r.dtype) for r in raw]
+        + [pltpu.SemaphoreType.DMA((5 + groups,))],
         compiler_params=params,
         name="prep",
-    )(*[pltpu.with_memory_space_constraint(r, pltpu.HBM) for r in raw])
-    own_keys = of_heads(sub_keys, mine)
+    )(*[pltpu.with_memory_space_constraint(r, pltpu.HBM) for r in (*raw, queries, sub_keys)])
+    tabs, cuts, own_keys = prepared[:groups], prepared[groups:-1], by_head(prepared[-1])
     keys = [own_keys] + [swap(own_keys, "key", nkey, e) for e in range(1, nkey)]
     tabs = [tabs[0]] + [swap(tabs[d], "dp", ndp, d) for d in range(1, groups)]
-    qs = [of_heads(queries, mine ^ d) for d in range(groups)]
+    qs = [by_head(cut) for cut in cuts]
     qs = [qs[0]] + [swap(qs[d], "dp", ndp, d) for d in range(1, groups)]
 
     def call(kernel, outs, *ins, scratch=()):
@@ -337,7 +345,10 @@
         [shape((units, blk, width), F32 if d == 0 else BF16) for d in range(groups)],
         *parts,
     )
-    pieces = [pieces[0]] + [swap(pieces[d], "dp", ndp, d) for d in range(1, groups)]
+    moved = [pieces[0]]
+    for d in range(1, groups):
+        moved.append(swap(pieces[d], "dp", ndp, d))
+    pieces = moved
     pieces = [p.astype(F32) for p in pieces]
     stacked = jnp.stack(pieces).reshape(groups, per, halves, blk, width)
     order = jnp.stack([lax.dynamic_index_in_dim(stacked, mine ^ d, 0, False) for d in range(groups)])
@@ -367,14 +378,7 @@
         scratch=[pltpu.VMEM((len(late) * span, tok), BF16)],
     )
     outs = [outs[0]] + [swap(outs[e], "tensor", ntensor, e) for e in range(1, ntensor)]
-    input_grad = pl.pallas_call(
-        join_kernel,
-        out_shape=jax.ShapeDtypeStruct((here, rows), BF16),
-        in_specs=[whole()] * ntensor,
-        out_specs=whole(),
-        compiler_params=params,
-        name="join",
-    )(*outs)
+    input_grad = call(join_kernel, shape((here, rows), BF16), *outs)
     return sub_key_grad, input_grad
 
 

time: 81 us -> 91.3 us (1.13)
  local copies, waits for them, and re-layouts: 3.59 us -> 12.9 us
  waiting for transfers between devices: 22.7 us -> 28.3 us
  Pallas kernels: 24 us -> 21.4 us
  starting transfers between devices: 29.5 us -> 27.5 us
    unnamed x10 -> x5, local copies, waits for them, and re-layouts: 1.36 us -> 12.7 us
    ppermute x20, waiting for transfers between devices: 22.7 us -> 28.3 us  [swap(): return lax.ppermute(x, axis, [(i, i ^ d) for i in range(size)])]
    dynamic_slice x2 -> x0, local copies, waits for them, and re-layouts: 2.18 us -> none  [of_heads(): lax.dynamic_slice_in_dim(array, first * per, per, 1)]
    ppermute x20, starting transfers between devices: 29.5 us -> 27.5 us  [swap(): return lax.ppermute(x, axis, [(i, i ^ d) for i in range(size)])]
    pallas_call x1 -> x0, Pallas kernels: 1.32 us -> none  [on_device(): pl.pallas_call(join_kernel, out_shape=jax.ShapeDtypeStruct((here, rows),...]
    pallas_call x11 -> x12, Pallas kernels: 20.2 us -> 18.9 us  [call(): pl.pallas_call(kernel, out_shape=outs, in_specs=[whole()] * len(ins), out...]
  transfers between devices with their start and end apart: 20 -> 20, of which waited for: 6 -> 7; matrix products, arithmetic and copies ran while one was open for 2% -> 2% of each run, Pallas kernels for 28% -> 19%
where the time goes in v3:
time: 91.3 us; the launch traced here: 91.1 us
  waiting for transfers between devices  28.3 us (31%)
  starting transfers between devices  27.5 us (30%)
  Pallas kernels  21.4 us (23%)
  local copies, waits for them, and re-layouts  12.9 us (14%)
    ppermute x20, waiting for transfers between devices, swap(): return lax.ppermute(x, axis, [(i, i ^ d) for i in range(size)])  28.3 us
    ppermute x20, starting transfers between devices, swap(): return lax.ppermute(x, axis, [(i, i ^ d) for i in range(size)])  27.5 us
    pallas_call x12, Pallas kernels, call(): pl.pallas_call(kernel, out_shape=outs, in_specs=[whole()] * len(ins), out...  18.9 us
    unnamed x5, local copies, waits for them, and re-layouts  12.7 us
    pallas_call x1, Pallas kernels, on_device(): pl.pallas_call(functools.partial(prep_kernel, groups, per, topk), out_sha...  2.54 us
  transfers between devices with their start and end apart: 20, of which 7 were waited for; matrix products, arithmetic and copies ran while one was open for 2% of the time, Pallas kernels for 19%

profile of v3, /device:TPU:0, one launch (start us, length us, event | category | flops | bytes accessed | tf_op | source)
XLA Modules:
  0.0 91.1 jit_solution(4598536995464077473)
XLA Ops:
  0.6 2.5 %prep.1 = (bf16[1,2,2,32,256]{4,3,2,1,0:T(8,128)(2,1)S(1)}, bf16[1,2,2,32,256]{4,3,2,1,0:T(8,128)(2,1)S(1)}, bf16[1,2,2,32,256]{4,3,2,1,0:T(8,128)(2,1)S(1)}, bf...) custom-call(s32[4,32,256]{2,1,0:T(8,128)} %bitcast.60, ...), custom_call_target="tpu_custom_call" | custom-call | tf_op jit(solution)/shard_map/prep/pallas_call | solution.py:240
  3.2 4.0 %collective-permute-start.5 = (bf16[1,2,256,256]{3,2,1,0:T(8,128)(2,1)S(1)}, bf16[1,2,256,256]{3,2,1,0:T(8,128)(2,1)S(1)}, u32[]{:S(2)}, u32[]{:S(2)}) collective-permute-start(bf16[1,2,256,256]{3,2,1,0:T(8,128)(2,1)S(1)} %bitcast.58), channel_id=1, source_target_pairs={{0,24},{8,16},{16,8},{24,0},{1,25},{9,17},{17,9},{25,1},{2,26},{10... | collective-permute-start | bytes 786440 | tf_op jit(solution)/shard_map/ppermute | solution.py:214
  8.0 1.9 %collective-permute-start = (bf16[1,2,2,32,256]{4,3,2,1,0:T(8,128)(2,1)S(1)}, bf16[1,2,2,32,256]{4,3,2,1,0:T(8,128)(2,1)S(1)}, u32[]{:S(2)}, u32[]{:S(2)}) collective-permute-start(bf16[1,2,2,32,256]{4,3,2,1,0:T(8,128)(2,1)S(1)} %get-tuple-element.33), channel_id=1, source_target_pairs={{0,8},{8,0},{16,24},{24,16},{1,9},{9,1},{17,25},{25,17},{2,10},{10... | collective-permute-start | bytes 196616 | tf_op jit(solution)/shard_map/ppermute | solution.py:214
  9.9 1.5 %collective-permute-start.1 = (bf16[1,2,2,32,256]{4,3,2,1,0:T(8,128)(2,1)S(1)}, bf16[1,2,2,32,256]{4,3,2,1,0:T(8,128)(2,1)S(1)}, u32[]{:S(2)}, u32[]{:S(2)}) collective-permute-start(bf16[1,2,2,32,256]{4,3,2,1,0:T(8,128)(2,1)S(1)} %get-tuple-element.34), channel_id=1, source_target_pairs={{0,16},{8,24},{16,0},{24,8},{1,17},{9,25},{17,1},{25,9},{2,18},{10... | collective-permute-start | bytes 196616 | tf_op jit(solution)/shard_map/ppermute | solution.py:214
  11.5 9.4 %collective-permute-done.refs_0_ = bf16[1,2,2,32,256]{4,3,2,1,0:T(8,128)(2,1)S(1)} collective-permute-done((bf16[1,2,2,32,256]{4,3,2,1,0:T(8,128)(2,1)S(1)}, bf16[1,2,2,32,256]{4,3,2,1,0:T(8,128)(2,1)S(1)}, u32[]{:S(2)}, u32[]{:S(2)}) %collective-permute-start) | collective-permute-done | bytes 65568 | tf_op jit(solution)/shard_map/ppermute | solution.py:214
  20.8 1.4 %collective-permute-start.2 = (bf16[1,2,2,32,256]{4,3,2,1,0:T(8,128)(2,1)S(1)}, bf16[1,2,2,32,256]{4,3,2,1,0:T(8,128)(2,1)S(1)}, u32[]{:S(2)}, u32[]{:S(2)}) collective-permute-start(bf16[1,2,2,32,256]{4,3,2,1,0:T(8,128)(2,1)S(1)} %get-tuple-element.35), channel_id=1, source_target_pairs={{0,24},{8,16},{16,8},{24,0},{1,25},{9,17},{17,9},{25,1},{2,26},{10... | collective-permute-start | bytes 196616 | tf_op jit(solution)/shard_map/ppermute | solution.py:214
  22.3 3.7 %collective-permute-start.15 = (bf16[1,2,256,256]{3,2,1,0:T(8,128)(2,1)S(1)}, bf16[1,2,256,256]{3,2,1,0:T(8,128)(2,1)S(1)}, u32[]{:S(2)}, u32[]{:S(2)}) collective-permute-start(bf16[1,2,256,256]{3,2,1,0:T(8,128)(2,1)S(1)} %bitcast.47), channel_id=1, source_target_pairs={{0,6},{2,4},{4,2},{6,0},{1,7},{3,5},{5,3},{7,1},{8,14},{10,12},{12... | collective-permute-start | bytes 786440 | tf_op jit(solution)/shard_map/ppermute | solution.py:214
  26.0 2.6 %collective-permute-start.14 = (bf16[1,2,256,256]{3,2,1,0:T(8,128)(2,1)S(1)}, bf16[1,2,256,256]{3,2,1,0:T(8,128)(2,1)S(1)}, u32[]{:S(2)}, u32[]{:S(2)}) collective-permute-start(bf16[1,2,256,256]{3,2,1,0:T(8,128)(2,1)S(1)} %bitcast.48), channel_id=1, source_target_pairs={{0,4},{2,6},{4,0},{6,2},{1,5},{3,7},{5,1},{7,3},{8,12},{10,14},{12... | collective-permute-start | bytes 786440 | tf_op jit(solution)/shard_map/ppermute | solution.py:214
  28.6 1.6 %collective-permute-start.13 = (bf16[1,2,256,256]{3,2,1,0:T(8,128)(2,1)S(1)}, bf16[1,2,256,256]{3,2,1,0:T(8,128)(2,1)S(1)}, u32[]{:S(2)}, u32[]{:S(2)}) collective-permute-start(bf16[1,2,256,256]{3,2,1,0:T(8,128)(2,1)S(1)} %bitcast.49), channel_id=1, source_target_pairs={{0,2},{2,0},{4,6},{6,4},{1,3},{3,1},{5,7},{7,5},{8,10},{10,8},{12,... | collective-permute-start | bytes 786440 | tf_op jit(solution)/shard_map/ppermute | solution.py:214
  30.2 2.6 %shard_map.86 = (bf16[1024,256]{1,0:T(8,128)(2,1)S(1)}, bf16[1024,256]{1,0:T(8,128)(2,1)S(1)}) custom-call(bf16[1,2,2,32,256]{4,3,2,1,0:T(8,128)(2,1)S(1)} %get-tuple-element.31.refs_0_), custom_call_target="tpu_custom_call" | custom-call | tf_op jit(solution)/shard_map/pallas_call | solution.py:260
  32.8 3.6 %shard_map.90.refs_1_.refs_3_ = bf16[1024,768]{1,0:T(8,128)(2,1)S(1)} custom-call(bf16[1,2,2,32,256]{4,3,2,1,0:T(8,128)(2,1)S(1)} %collective-permute-done.refs_0_, bf16[1,2,2,32,256]{4,3,2,1,0:T(8,128)(2,1)S(1)} %collective-permute-done.1.refs_1_, bf16[1,2,2,32,256]{4,3,2,1,0:T(8,128)(2,1)S(1)} %collective-permute-done.2.refs_2_), custom_call_target="tpu_custom_call" | custom-call | tf_op jit(solution)/shard_map/pallas_call | solution.py:260
  37.8 3.6 %shard_map.87.refs_1_ = bf16[1024,768]{1,0:T(8,128)(2,1)S(1)} custom-call(bf16[1,2,2,32,256]{4,3,2,1,0:T(8,128)(2,1)S(1)} %collective-permute-done.refs_0_, bf16[1,2,2,32,256]{4,3,2,1,0:T(8,128)(2,1)S(1)} %collective-permute-done.1.refs_1_, bf16[1,2,2,32,256]{4,3,2,1,0:T(8,128)(2,1)S(1)} %collective-permute-done.2.refs_2_), custom_call_target="tpu_custom_call" | custom-call | tf_op jit(solution)/shard_map/pallas_call | solution.py:260
  42.2 1.6 %collective-permute-start.6 = (bf16[2,4,64,256]{3,2,1,0:T(8,128)(2,1)S(1)}, bf16[2,4,64,256]{3,2,1,0:T(8,128)(2,1)S(1)}, u32[]{:S(2)}, u32[]{:S(2)}) collective-permute-start(bf16[2,4,64,256]{3,2,1,0:T(8,128)(2,1)S(1)} %get-tuple-element.41), channel_id=1, source_target_pairs={{0,2},{2,0},{4,6},{6,4},{1,3},{3,1},{5,7},{7,5},{8,10},{10,8},{12,... | collective-permute-start | bytes 786440 | tf_op jit(solution)/shard_map/ppermute | solution.py:214
  43.9 3.4 %collective-permute-done.14.refs_6_ = bf16[1,2,256,256]{3,2,1,0:T(8,128)(2,1)S(1)} collective-permute-done((bf16[1,2,256,256]{3,2,1,0:T(8,128)(2,1)S(1)}, bf16[1,2,256,256]{3,2,1,0:T(8,128)(2,1)S(1)}, u32[]{:S(2)}, u32[]{:S(2)}) %collective-permute-start.14) | collective-permute-done | bytes 262176 | tf_op jit(solution)/shard_map/ppermute | solution.py:214
  50.6 1.4 %collective-permute-start.18 = (bf16[1,2,256,256]{3,2,1,0:T(8,128)(2,1)S(1)}, bf16[1,2,256,256]{3,2,1,0:T(8,128)(2,1)S(1)}, u32[]{:S(2)}, u32[]{:S(2)}) collective-permute-start(bf16[1,2,256,256]{3,2,1,0:T(8,128)(2,1)S(1)} %get-tuple-element.56), channel_id=1, source_target_pairs={{0,24},{8,16},{16,8},{24,0},{1,25},{9,17},{17,9},{25,1},{2,26},{10... | collective-permute-start | bytes 786440 | tf_op jit(solution)/shard_map/ppermute | solution.py:214
  52.2 4.0 %collective-permute-done.6.got = bf16[2,4,64,256]{3,2,1,0:T(8,128)(2,1)S(1)} collective-permute-done((bf16[2,4,64,256]{3,2,1,0:T(8,128)(2,1)S(1)}, bf16[2,4,64,256]{3,2,1,0:T(8,128)(2,1)S(1)}, u32[]{:S(2)}, u32[]{:S(2)}) %collective-permute-start.6) | collective-permute-done | bytes 262176 | tf_op jit(solution)/shard_map/ppermute | solution.py:214
  56.9 6.4 %collective-permute-done.9 = bf16[1,4,64,256]{3,2,1,0:T(8,128)(2,1)S(1)} collective-permute-done((bf16[1,4,64,256]{3,2,1,0:T(8,128)(2,1)S(1)}, bf16[1,4,64,256]{3,2,1,0:T(8,128)(2,1)S(1)}, u32[]{:S(2)}, u32[]{:S(2)}) %collective-permute-start.9) | collective-permute-done | bytes 131104 | tf_op jit(solution)/shard_map/ppermute | solution.py:214
  63.2 1.4 %collective-permute-done.7 = bf16[1,4,64,256]{3,2,1,0:T(8,128)(2,1)S(1)} collective-permute-done((bf16[1,4,64,256]{3,2,1,0:T(8,128)(2,1)S(1)}, bf16[1,4,64,256]{3,2,1,0:T(8,128)(2,1)S(1)}, u32[]{:S(2)}, u32[]{:S(2)}) %collective-permute-start.7) | collective-permute-done | bytes 131104 | tf_op jit(solution)/shard_map/ppermute | solution.py:214
  66.1 5.8 %copy-done = bf16[4096,2048]{1,0:T(8,128)(2,1)S(1)} copy-done((bf16[4096,2048]{1,0:T(8,128)(2,1)S(1)}, bf16[4096,2048]{1,0:T(8,128)(2,1)}, u32[]{:S(2)}) %copy-start) | copy-done | bytes 16777240
  73.1 5.8 %copy-done.1 = bf16[4096,2048]{1,0:T(8,128)(2,1)S(1)} copy-done((bf16[4096,2048]{1,0:T(8,128)(2,1)S(1)}, bf16[4096,2048]{1,0:T(8,128)(2,1)}, u32[]{:S(2)}) %copy-start.1) | copy-done | bytes 16777240
  78.9 3.5 %shard_map.96 = (f32[4096,128]{1,0:T(8,128)S(1)}, bf16[4096,128]{1,0:T(8,128)(2,1)S(1)}) custom-call(bf16[1,2,256,256]{3,2,1,0:T(8,128)(2,1)S(1)} %collective-permute-done.16.refs_0_, bf16[1,2,256,256]{3,2,1,0:T(8,128)(2,1)S(1)} %collective-permute-done.17.refs_1_, bf16[1,2,256,256]{3,2,1,0:T(8,128)(2,1)S(1)} %collective-permute-done.18.refs_2_, ...), custom_call_target="tpu_custom_call" | custom-call | tf_op jit(solution)/shard_map/pallas_call | solution.py:260
  83.2 1.4 %collective-permute-start.12 = (bf16[2,64,256]{2,1,0:T(8,128)(2,1)S(1)}, bf16[2,64,256]{2,1,0:T(8,128)(2,1)S(1)}, u32[]{:S(2)}, u32[]{:S(2)}) collective-permute-start(bf16[2,64,256]{2,1,0:T(8,128)(2,1)S(1)} %get-tuple-element.52), channel_id=1, source_target_pairs={{0,24},{8,16},{16,8},{24,0},{1,25},{9,17},{17,9},{25,1},{2,26},{10... | collective-permute-start | bytes 196616 | tf_op jit(solution)/shard_map/ppermute | solution.py:214
  84.6 2.3 %collective-permute-done.11 = bf16[2,64,256]{2,1,0:T(8,128)(2,1)S(1)} collective-permute-done((bf16[2,64,256]{2,1,0:T(8,128)(2,1)S(1)}, bf16[2,64,256]{2,1,0:T(8,128)(2,1)S(1)}, u32[]{:S(2)}, u32[]{:S(2)}) %collective-permute-start.11) | collective-permute-done | bytes 65568 | tf_op jit(solution)/shard_map/ppermute | solution.py:214
  86.9 1.5 %collective-permute-done.12 = bf16[2,64,256]{2,1,0:T(8,128)(2,1)S(1)} collective-permute-done((bf16[2,64,256]{2,1,0:T(8,128)(2,1)S(1)}, bf16[2,64,256]{2,1,0:T(8,128)(2,1)S(1)}, u32[]{:S(2)}, u32[]{:S(2)}) %collective-permute-start.12) | collective-permute-done | bytes 65568 | tf_op jit(solution)/shard_map/ppermute | solution.py:214
  (45 shorter events, 13.4 us)
Async XLA Ops:
  3.2 25.4 %collective-permute-start.5 = (bf16[1,2,256,256]{3,2,1,0:T(8,128)(2,1)S(1)}, bf16[1,2,256,256]{3,2,1,0:T(8,128)(2,1)S(1)}, u32[]{:S(2)}, u32[]{:S(2)}) collective-permute-start(bf16[1,2,256,256]{3,2,1,0:T(8,128)(2,1)S(1)} %bitcast.58), channel_id=1, source_target_pairs={{0,24},{8,16},{16,8},{24,0},{1,25},{9,17},{17,9},{25,1},{2,26},{10... | collective-permute-start | bytes 786440 | tf_op jit(solution)/shard_map/ppermute | solution.py:214
  7.2 29.3 %collective-permute-start.4 = (bf16[1,2,256,256]{3,2,1,0:T(8,128)(2,1)S(1)}, bf16[1,2,256,256]{3,2,1,0:T(8,128)(2,1)S(1)}, u32[]{:S(2)}, u32[]{:S(2)}) collective-permute-start(bf16[1,2,256,256]{3,2,1,0:T(8,128)(2,1)S(1)} %bitcast.56), channel_id=1, source_target_pairs={{0,16},{8,24},{16,0},{24,8},{1,17},{9,25},{17,1},{25,9},{2,18},{10... | collective-permute-start | bytes 786440 | tf_op jit(solution)/shard_map/ppermute | solution.py:214
  7.8 28.7 %collective-permute-start.3 = (bf16[1,2,256,256]{3,2,1,0:T(8,128)(2,1)S(1)}, bf16[1,2,256,256]{3,2,1,0:T(8,128)(2,1)S(1)}, u32[]{:S(2)}, u32[]{:S(2)}) collective-permute-start(bf16[1,2,256,256]{3,2,1,0:T(8,128)(2,1)S(1)} %bitcast.57), channel_id=1, source_target_pairs={{0,8},{8,0},{16,24},{24,16},{1,9},{9,1},{17,25},{25,17},{2,10},{10... | collective-permute-start | bytes 786440 | tf_op jit(solution)/shard_map/ppermute | solution.py:214
  8.0 12.8 %collective-permute-start = (bf16[1,2,2,32,256]{4,3,2,1,0:T(8,128)(2,1)S(1)}, bf16[1,2,2,32,256]{4,3,2,1,0:T(8,128)(2,1)S(1)}, u32[]{:S(2)}, u32[]{:S(2)}) collective-permute-start(bf16[1,2,2,32,256]{4,3,2,1,0:T(8,128)(2,1)S(1)} %get-tuple-element.33), channel_id=1, source_target_pairs={{0,8},{8,0},{16,24},{24,16},{1,9},{9,1},{17,25},{25,17},{2,10},{10... | collective-permute-start | bytes 196616 | tf_op jit(solution)/shard_map/ppermute | solution.py:214
  9.9 12.4 %collective-permute-start.1 = (bf16[1,2,2,32,256]{4,3,2,1,0:T(8,128)(2,1)S(1)}, bf16[1,2,2,32,256]{4,3,2,1,0:T(8,128)(2,1)S(1)}, u32[]{:S(2)}, u32[]{:S(2)}) collective-permute-start(bf16[1,2,2,32,256]{4,3,2,1,0:T(8,128)(2,1)S(1)} %get-tuple-element.34), channel_id=1, source_target_pairs={{0,16},{8,24},{16,0},{24,8},{1,17},{9,25},{17,1},{25,9},{2,18},{10... | collective-permute-start | bytes 196616 | tf_op jit(solution)/shard_map/ppermute | solution.py:214
  20.8 5.2 %collective-permute-start.2 = (bf16[1,2,2,32,256]{4,3,2,1,0:T(8,128)(2,1)S(1)}, bf16[1,2,2,32,256]{4,3,2,1,0:T(8,128)(2,1)S(1)}, u32[]{:S(2)}, u32[]{:S(2)}) collective-permute-start(bf16[1,2,2,32,256]{4,3,2,1,0:T(8,128)(2,1)S(1)} %get-tuple-element.35), channel_id=1, source_target_pairs={{0,24},{8,16},{16,8},{24,0},{1,25},{9,17},{17,9},{25,1},{2,26},{10... | collective-permute-start | bytes 196616 | tf_op jit(solution)/shard_map/ppermute | solution.py:214
  22.3 21.6 %collective-permute-start.15 = (bf16[1,2,256,256]{3,2,1,0:T(8,128)(2,1)S(1)}, bf16[1,2,256,256]{3,2,1,0:T(8,128)(2,1)S(1)}, u32[]{:S(2)}, u32[]{:S(2)}) collective-permute-start(bf16[1,2,256,256]{3,2,1,0:T(8,128)(2,1)S(1)} %bitcast.47), channel_id=1, source_target_pairs={{0,6},{2,4},{4,2},{6,0},{1,7},{3,5},{5,3},{7,1},{8,14},{10,12},{12... | collective-permute-start | bytes 786440 | tf_op jit(solution)/shard_map/ppermute | solution.py:214
  26.0 21.3 %collective-permute-start.14 = (bf16[1,2,256,256]{3,2,1,0:T(8,128)(2,1)S(1)}, bf16[1,2,256,256]{3,2,1,0:T(8,128)(2,1)S(1)}, u32[]{:S(2)}, u32[]{:S(2)}) collective-permute-start(bf16[1,2,256,256]{3,2,1,0:T(8,128)(2,1)S(1)} %bitcast.48), channel_id=1, source_target_pairs={{0,4},{2,6},{4,0},{6,2},{1,5},{3,7},{5,1},{7,3},{8,12},{10,14},{12... | collective-permute-start | bytes 786440 | tf_op jit(solution)/shard_map/ppermute | solution.py:214
  28.6 18.7 %collective-permute-start.13 = (bf16[1,2,256,256]{3,2,1,0:T(8,128)(2,1)S(1)}, bf16[1,2,256,256]{3,2,1,0:T(8,128)(2,1)S(1)}, u32[]{:S(2)}, u32[]{:S(2)}) collective-permute-start(bf16[1,2,256,256]{3,2,1,0:T(8,128)(2,1)S(1)} %bitcast.49), channel_id=1, source_target_pairs={{0,2},{2,0},{4,6},{6,4},{1,3},{3,1},{5,7},{7,5},{8,10},{10,8},{12,... | collective-permute-start | bytes 786440 | tf_op jit(solution)/shard_map/ppermute | solution.py:214
  37.3 14.8 %collective-permute-start.8 = (bf16[2,4,64,256]{3,2,1,0:T(8,128)(2,1)S(1)}, bf16[2,4,64,256]{3,2,1,0:T(8,128)(2,1)S(1)}, u32[]{:S(2)}, u32[]{:S(2)}) collective-permute-start(bf16[2,4,64,256]{3,2,1,0:T(8,128)(2,1)S(1)} %get-tuple-element.46), channel_id=1, source_target_pairs={{0,2},{2,0},{4,6},{6,4},{1,3},{3,1},{5,7},{7,5},{8,10},{10,8},{12,... | collective-permute-start | bytes 786440 | tf_op jit(solution)/shard_map/ppermute | solution.py:214
  42.2 14.0 %collective-permute-start.6 = (bf16[2,4,64,256]{3,2,1,0:T(8,128)(2,1)S(1)}, bf16[2,4,64,256]{3,2,1,0:T(8,128)(2,1)S(1)}, u32[]{:S(2)}, u32[]{:S(2)}) collective-permute-start(bf16[2,4,64,256]{3,2,1,0:T(8,128)(2,1)S(1)} %get-tuple-element.41), channel_id=1, source_target_pairs={{0,2},{2,0},{4,6},{6,4},{1,3},{3,1},{5,7},{7,5},{8,10},{10,8},{12,... | collective-permute-start | bytes 786440 | tf_op jit(solution)/shard_map/ppermute | solution.py:214
  48.5 24.5 %collective-permute-start.16 = (bf16[1,2,256,256]{3,2,1,0:T(8,128)(2,1)S(1)}, bf16[1,2,256,256]{3,2,1,0:T(8,128)(2,1)S(1)}, u32[]{:S(2)}, u32[]{:S(2)}) collective-permute-start(bf16[1,2,256,256]{3,2,1,0:T(8,128)(2,1)S(1)} %get-tuple-element.54), channel_id=1, source_target_pairs={{0,8},{8,0},{16,24},{24,16},{1,9},{9,1},{17,25},{25,17},{2,10},{10... | collective-permute-start | bytes 786440 | tf_op jit(solution)/shard_map/ppermute | solution.py:214
  49.8 23.3 %collective-permute-start.17 = (bf16[1,2,256,256]{3,2,1,0:T(8,128)(2,1)S(1)}, bf16[1,2,256,256]{3,2,1,0:T(8,128)(2,1)S(1)}, u32[]{:S(2)}, u32[]{:S(2)}) collective-permute-start(bf16[1,2,256,256]{3,2,1,0:T(8,128)(2,1)S(1)} %get-tuple-element.55), channel_id=1, source_target_pairs={{0,16},{8,24},{16,0},{24,8},{1,17},{9,25},{17,1},{25,9},{2,18},{10... | collective-permute-start | bytes 786440 | tf_op jit(solution)/shard_map/ppermute | solution.py:214
  50.6 22.5 %collective-permute-start.18 = (bf16[1,2,256,256]{3,2,1,0:T(8,128)(2,1)S(1)}, bf16[1,2,256,256]{3,2,1,0:T(8,128)(2,1)S(1)}, u32[]{:S(2)}, u32[]{:S(2)}) collective-permute-start(bf16[1,2,256,256]{3,2,1,0:T(8,128)(2,1)S(1)} %get-tuple-element.56), channel_id=1, source_target_pairs={{0,24},{8,16},{16,8},{24,0},{1,25},{9,17},{17,9},{25,1},{2,26},{10... | collective-permute-start | bytes 786440 | tf_op jit(solution)/shard_map/ppermute | solution.py:214
  52.1 11.1 %collective-permute-start.9 = (bf16[1,4,64,256]{3,2,1,0:T(8,128)(2,1)S(1)}, bf16[1,4,64,256]{3,2,1,0:T(8,128)(2,1)S(1)}, u32[]{:S(2)}, u32[]{:S(2)}) collective-permute-start(bf16[1,4,64,256]{3,2,1,0:T(8,128)(2,1)S(1)} %get-tuple-element.48), channel_id=1, source_target_pairs={{0,4},{2,6},{4,0},{6,2},{1,5},{3,7},{5,1},{7,3},{8,12},{10,14},{12... | collective-permute-start | bytes 393224 | tf_op jit(solution)/shard_map/ppermute | solution.py:214
  56.3 8.4 %collective-permute-start.7 = (bf16[1,4,64,256]{3,2,1,0:T(8,128)(2,1)S(1)}, bf16[1,4,64,256]{3,2,1,0:T(8,128)(2,1)S(1)}, u32[]{:S(2)}, u32[]{:S(2)}) collective-permute-start(bf16[1,4,64,256]{3,2,1,0:T(8,128)(2,1)S(1)} %get-tuple-element.43), channel_id=1, source_target_pairs={{0,4},{2,6},{4,0},{6,2},{1,5},{3,7},{5,1},{7,3},{8,12},{10,14},{12... | collective-permute-start | bytes 393224 | tf_op jit(solution)/shard_map/ppermute | solution.py:214
  64.7 19.9 %collective-permute-start.10 = (bf16[2,64,256]{2,1,0:T(8,128)(2,1)S(1)}, bf16[2,64,256]{2,1,0:T(8,128)(2,1)S(1)}, u32[]{:S(2)}, u32[]{:S(2)}) collective-permute-start(bf16[2,64,256]{2,1,0:T(8,128)(2,1)S(1)} %get-tuple-element.50), channel_id=1, source_target_pairs={{0,8},{8,0},{16,24},{24,16},{1,9},{9,1},{17,25},{25,17},{2,10},{10... | collective-permute-start | bytes 196616 | tf_op jit(solution)/shard_map/ppermute | solution.py:214
  66.1 5.8 %copy-start = (bf16[4096,2048]{1,0:T(8,128)(2,1)S(1)}, bf16[4096,2048]{1,0:T(8,128)(2,1)}, u32[]{:S(2)}) copy-start(bf16[4096,2048]{1,0:T(8,128)(2,1)} %refs_3_.1) | copy-start | bytes 50331652
  73.1 5.8 %copy-start.1 = (bf16[4096,2048]{1,0:T(8,128)(2,1)S(1)}, bf16[4096,2048]{1,0:T(8,128)(2,1)}, u32[]{:S(2)}) copy-start(bf16[4096,2048]{1,0:T(8,128)(2,1)} %refs_3_.1) | copy-start | bytes 50331652
  82.3 7.4 %collective-permute-start.19 = (bf16[4096,128]{1,0:T(8,128)(2,1)S(1)}, bf16[4096,128]{1,0:T(8,128)(2,1)S(1)}, u32[]{:S(2)}, u32[]{:S(2)}) collective-permute-start(bf16[4096,128]{1,0:T(8,128)(2,1)S(1)} %get-tuple-element.59), channel_id=1, source_target_pairs={{0,1},{1,0},{2,3},{3,2},{4,5},{5,4},{6,7},{7,6},{8,9},{9,8},{10,11... | collective-permute-start | bytes 3145736 | tf_op jit(solution)/shard_map/ppermute | solution.py:214
  82.4 4.5 %collective-permute-start.11 = (bf16[2,64,256]{2,1,0:T(8,128)(2,1)S(1)}, bf16[2,64,256]{2,1,0:T(8,128)(2,1)S(1)}, u32[]{:S(2)}, u32[]{:S(2)}) collective-permute-start(bf16[2,64,256]{2,1,0:T(8,128)(2,1)S(1)} %get-tuple-element.51), channel_id=1, source_target_pairs={{0,16},{8,24},{16,0},{24,8},{1,17},{9,25},{17,1},{25,9},{2,18},{10... | collective-permute-start | bytes 196616 | tf_op jit(solution)/shard_map/ppermute | solution.py:214
  83.2 5.2 %collective-permute-start.12 = (bf16[2,64,256]{2,1,0:T(8,128)(2,1)S(1)}, bf16[2,64,256]{2,1,0:T(8,128)(2,1)S(1)}, u32[]{:S(2)}, u32[]{:S(2)}) collective-permute-start(bf16[2,64,256]{2,1,0:T(8,128)(2,1)S(1)} %get-tuple-element.52), channel_id=1, source_target_pairs={{0,24},{8,16},{16,8},{24,0},{1,25},{9,17},{17,9},{25,1},{2,26},{10... | collective-permute-start | bytes 196616 | tf_op jit(solution)/shard_map/ppermute | solution.py:214
